TPU v7x, 128 devices: a whole 4x4x4 slice. The times are simulated.
128 devices in a mesh: dp: 128 (over x, z, y, core).
Axes of the slice: x: 4, y: 4, z: 4, core: 2. Of those that a mesh axis runs over, the one named last changes fastest.
Arguments:
- hidden: bfloat16 [98304, 2560], P('dp'), may hold values from -16 to 16
- rotation: bfloat16 [2560, 2560], P('dp'), may hold values from -1 to 1, as said below
- norm_gain: float32 [2, 2560], replicated, may hold values from 0.1 to 1.9
- value_weight: bfloat16 [2, 2560, 1024], P(None, None, 'dp'), may hold values from -0.125 to 0.125
- output_weight: bfloat16 [2, 1024, 2560], P(None, 'dp'), may hold values from -0.1875 to 0.1875
- lengths: int32 [128], replicated, may hold values from 1 to 768, as said below
Outputs:
- rotated_out: bfloat16 [98304, 2560], P('dp')
- calib_loss: float32 [], replicated
Inputs may be any that keep to these rules, and one draw needn't show every extreme that they name: `lengths`: some device has all of its 768 rows live. `rotation`: an orthogonal matrix rounded to bfloat16.
All inputs are finite; a program needn't handle non-finite values.
Results may differ from a plain program's by a relative error of at most 0.0088.
Values may be sent and summed in bfloat16 or wider, within the bound.
A program may use at most 192 MiB of HBM per device.

v0:
```python
import functools

import jax
import jax.numpy as jnp
from jax import lax
from jax.sharding import Mesh
from jax.sharding import PartitionSpec as P

BLOCK = 256
SLOTS = 3
DP = ("dp_0", "dp_1", "dp_2", "dp_3")


EPS_NORM = 1e-06
EPS_SCALE = 1e-06
CLIP_RATIO = 0.9
TWO_PI = 6.283185307179586


def one_axis_at_a_time(x, axes):
    for axis in axes:
        x = lax.pmax(x, axis)
    return x


def over_pieces(x, axis):
    return lax.all_gather(x, axis).max(0)


def over_axes(x, axes):
    return functools.reduce(lax.psum, axes, x)


def soft_round(values):
    return values - jnp.sin(TWO_PI * values) / TWO_PI


def fake_quant(values, step_size):
    return soft_round(jnp.clip(values / step_size, -8.0, 7.0)) * step_size


def quantize_with(matrix, column_tops):
    return fake_quant(matrix, column_tops / 7.0 + EPS_SCALE).astype(jnp.bfloat16)


def rotate_weights(rotation_full, norm_gain, value_weight, output_weight):
    layer_count = norm_gain.shape[0]
    value_cols = value_weight.shape[2]
    output_rows = output_weight.shape[1]
    pieces = []
    for number in range(layer_count):
        scaled = (norm_gain[number][:, None] * value_weight[number].astype(jnp.float32)).astype(
            jnp.bfloat16
        )
        pieces.append(scaled)
        pieces.append(jnp.transpose(output_weight[number]))
    joined = jnp.concatenate(pieces, axis=1)
    product = lax.dot_general(
        rotation_full, joined, (((0,), (0,)), ((), ())), preferred_element_type=jnp.float32
    )
    value_list = []
    output_list = []
    offset = 0
    for number in range(layer_count):
        rotated_v = product[:, offset : offset + value_cols]
        value_list.append(quantize_with(rotated_v, jnp.max(jnp.abs(rotated_v), axis=0)[None, :]))
        offset = offset + value_cols
        output_list.append(jnp.transpose(product[:, offset : offset + output_rows]))
        offset = offset + output_rows
    return (value_list, output_list)


def per_device(hidden, rotation, norm_gain, value_weight, output_weight, lengths):
    own_index = lax.axis_index(DP)
    width = hidden.shape[1]
    layer_count = norm_gain.shape[0]
    rotation_full = lax.all_gather(rotation, DP, axis=0, tiled=True)
    value_list, output_list = rotate_weights(rotation_full, norm_gain, value_weight, output_weight)
    value_local = jnp.stack(value_list)
    output_local = jnp.stack(output_list)
    output_tops = one_axis_at_a_time(jnp.max(jnp.abs(output_local), axis=1), DP)
    value_all = lax.all_gather(value_local, DP, axis=2, tiled=True)
    output_all = lax.all_gather(
        quantize_with(output_local, output_tops[:, None, :]), DP, axis=1, tiled=True
    )
    own_len = lax.dynamic_index_in_dim(lengths, own_index, 0, keepdims=False)
    own_blocks = (own_len + BLOCK - 1) // BLOCK
    x_blocks = hidden.reshape(SLOTS, BLOCK, width)
    slot_range = jnp.arange(SLOTS, dtype=jnp.int32)
    own_valid = jnp.clip(own_len - slot_range * BLOCK, 0, BLOCK)
    done_slots = slot_range < own_blocks
    work_slots = x_blocks.shape[0]
    active = (jnp.arange(BLOCK, dtype=jnp.int32)[None, :] < own_valid[:, None]) & done_slots[
        :, None
    ]

    def slot_of(step_number):
        return jnp.where(step_number < own_blocks, step_number, SLOTS + step_number - own_blocks)

    def rotate_step(step_number, resid_buf):
        slot_pos = slot_of(step_number)
        block_rows = lax.dynamic_index_in_dim(x_blocks, slot_pos, 0, keepdims=False)
        rotated = jnp.dot(block_rows, rotation_full, preferred_element_type=jnp.float32)
        return lax.dynamic_update_index_in_dim(resid_buf, rotated, slot_pos, 0)

    resid_buf = lax.fori_loop(
        0, own_blocks, rotate_step, jnp.zeros((work_slots, BLOCK, width), jnp.float32)
    )
    local_loss = jnp.zeros((), jnp.float32)
    for layer_number in range(layer_count):
        value_q = value_all[layer_number]
        output_q = output_all[layer_number]
        channels = value_q.shape[1]

        def first_step(step_number, carry):
            square_buf, error_buf, mixed_buf, channel_top = carry
            slot_pos = slot_of(step_number)
            residual = lax.dynamic_index_in_dim(resid_buf, slot_pos, 0, keepdims=False)
            live_mask = lax.dynamic_index_in_dim(active, slot_pos, 0, keepdims=False)
            mean_sq = jnp.mean(residual * residual, axis=1)
            normed = residual * lax.rsqrt(mean_sq + EPS_NORM)[:, None]
            step_size = CLIP_RATIO * jnp.max(jnp.abs(normed), axis=1) / 7.0 + EPS_SCALE
            act_f = fake_quant(normed, step_size[:, None])
            act_err = jnp.sum((act_f - normed) * (act_f - normed), axis=1)
            mixed = jnp.dot(act_f.astype(jnp.bfloat16), value_q, preferred_element_type=jnp.float32)
            channel_top = jnp.maximum(
                channel_top, jnp.max(jnp.where(live_mask[:, None], jnp.abs(mixed), 0.0), axis=0)
            )
            square_buf = lax.dynamic_update_index_in_dim(square_buf, mean_sq, slot_pos, 0)
            error_buf = lax.dynamic_update_index_in_dim(error_buf, act_err, slot_pos, 0)
            mixed_buf = lax.dynamic_update_index_in_dim(mixed_buf, mixed, slot_pos, 0)
            return (square_buf, error_buf, mixed_buf, channel_top)

        first_init = (
            jnp.zeros((work_slots, BLOCK), jnp.float32),
            jnp.zeros((work_slots, BLOCK), jnp.float32),
            jnp.zeros((work_slots, BLOCK, channels), jnp.float32),
            jnp.zeros((channels,), jnp.float32),
        )
        square_buf, error_buf, mixed_buf, channel_top = lax.fori_loop(
            0, own_blocks, first_step, first_init
        )
        vrange = over_pieces(channel_top, DP)
        mix_step = CLIP_RATIO * vrange / 7.0 + EPS_SCALE

        def second_step(step_number, carry):
            residual_all, mix_error_buf = carry
            slot_pos = slot_of(step_number)
            residual = lax.dynamic_index_in_dim(residual_all, slot_pos, 0, keepdims=False)
            mixed = lax.dynamic_index_in_dim(mixed_buf, slot_pos, 0, keepdims=False)
            mix_f = fake_quant(mixed, mix_step[None, :])
            mix_err = jnp.sum((mix_f - mixed) * (mix_f - mixed), axis=1)
            updated = residual + jnp.dot(
                mix_f.astype(jnp.bfloat16), output_q, preferred_element_type=jnp.float32
            )
            residual_all = lax.dynamic_update_index_in_dim(residual_all, updated, slot_pos, 0)
            mix_error_buf = lax.dynamic_update_index_in_dim(mix_error_buf, mix_err, slot_pos, 0)
            return (residual_all, mix_error_buf)

        resid_buf, mix_error_buf = lax.fori_loop(
            0, own_blocks, second_step, (resid_buf, jnp.zeros((work_slots, BLOCK), jnp.float32))
        )
        local_loss = local_loss + jnp.sum(
            jnp.where(active, square_buf * (error_buf + mix_error_buf), 0.0)
        )
    out_work = jnp.where(active[:, :, None], resid_buf, 0.0).astype(jnp.bfloat16)
    loss_sum = over_axes(local_loss, DP)
    count = jnp.sum(lengths).astype(jnp.float32)
    return (out_work.reshape(SLOTS * BLOCK, width), loss_sum / count)


def solution(mesh):
    finer = Mesh(mesh.devices.reshape(4, 4, 4, 2), ("dp_0", "dp_1", "dp_2", "dp_3"))
    in_specs = (P(DP, None), P(DP, None), P(), P(None, None, DP), P(None, DP, None), P())
    out_specs = (P(DP, None), P())
    return jax.shard_map(
        per_device, mesh=finer, in_specs=in_specs, out_specs=out_specs, check_vma=False
    )
```

profile of v0, /device:TPU:0, one launch (start us, length us, event | category | flops | bytes accessed | tf_op | source)
XLA Modules:
  0.0 626.4 jit_solution(12356554069797216184)
XLA Ops:
  10.4 81.2 %all-gather.11.cloned.1.call-done = bf16[128,20,2560]{2,1,0:T(8,128)(2,1)} async-done(((bf16[1,20,2560]{2,1,0:T(8,128)(2,1)}), bf16[128,20,2560]{2,1,0:T(8,128)(2,1)}) %all-gather.11.cloned.1.call-update) | async-done | bytes 13107216 | tf_op jit(solution)/shard_map/all_gather | solution.py:77
  91.6 18.0 %reshape.135 = bf16[2560,2560]{1,0:T(8,128)(2,1)} reshape(bf16[128,20,2560]{2,1,0:T(8,128)(2,1)} %all-gather.11.cloned.1.call-done) | data formatting | bytes 26214400
  118.3 16.9 %pmax.28 = f32[2,2560]{1,0:T(2,128)S(1)} all-reduce(f32[2,2560]{1,0:T(2,128)S(1)} %abs_reduce_fusion.2), channel_id=1, replica_groups=mesh['dp_0'=4,'dp_1'=4,'dp_2'=4,'dp_3'=2] {'dp_0'}, use_global_device_ids=true, to_apply=%region_12.13 | all-reduce | flops 5120 | bytes 40960 | tf_op jit(solution)/shard_map/pmax | solution.py:22
  135.2 16.6 %pmax.29 = f32[2,2560]{1,0:T(2,128)S(1)} all-reduce(f32[2,2560]{1,0:T(2,128)S(1)} %pmax.28), channel_id=1, replica_groups=mesh['dp_0'=4,'dp_1'=4,'dp_2'=4,'dp_3'=2] {'dp_1'}, use_global_device_ids=true, to_apply=%region_13.14 | all-reduce | flops 5120 | bytes 40960 | tf_op jit(solution)/shard_map/pmax | solution.py:22
  151.8 15.3 %pmax.30 = f32[2,2560]{1,0:T(2,128)S(1)} all-reduce(f32[2,2560]{1,0:T(2,128)S(1)} %pmax.29), channel_id=1, replica_groups=mesh['dp_0'=4,'dp_1'=4,'dp_2'=4,'dp_3'=2] {'dp_2'}, use_global_device_ids=true, to_apply=%region_14.15 | all-reduce | flops 5120 | bytes 40960 | tf_op jit(solution)/shard_map/pmax | solution.py:22
  179.0 21.2 %while.70 = (s32[]{:T(128)}, f32[3,256,2560]{2,1,0:T(8,128)}, s32[]{:T(128)}, bf16[3,256,2560]{2,1,0:T(8,128)(2,1)}, bf16[2560,2560]{1,0:T(8,128)(2,1)}, /*index=5*/s32[]{:T(128)}, s32[]{:T(128)}, s32[]{:T(128)}) while((s32[]{:T(128)}, f32[3,256,2560]{2,1,0:T(8,128)}, s32[]{:T(128)}, bf16[3,256,2560]{2,1,0:T(8,128)(2,1)}, ...), condition=%wide.region_1.2_spmd, body=%wide.region_0.0_spmd.sunk | while | flops 3355443200 | bytes 17040556 | solution.py:106
  179.0 11.0 %fusion.58 = f32[3,256,2560]{2,1,0:T(8,128)} fusion(f32[3,256,2560]{2,1,0:T(8,128)} %get-tuple-element.790, s32[]{:T(128)S(6)} %select_n.121, bf16[2560,2560]{1,0:T(8,128)(2,1)} %get-tuple-element.801, bf16[3,256,2560]{2,1,0:T(8,128)(2,1)} %get-tuple-element.800), kind=kOutput, calls=%fused_computation.1.clone.1 | convolution fusion | flops 3355443200 | bytes 17040384 | tf_op jit(solution)/shard_map/while/body/dot_general | solution.py:103
  190.0 10.2 %fusion.58 = f32[3,256,2560]{2,1,0:T(8,128)} fusion(f32[3,256,2560]{2,1,0:T(8,128)} %get-tuple-element.790, s32[]{:T(128)S(6)} %select_n.121, bf16[2560,2560]{1,0:T(8,128)(2,1)} %get-tuple-element.801, bf16[3,256,2560]{2,1,0:T(8,128)(2,1)} %get-tuple-element.800), kind=kOutput, calls=%fused_computation.1.clone.1 | convolution fusion | flops 3355443200 | bytes 17040384 | tf_op jit(solution)/shard_map/while/body/dot_general | solution.py:103
  217.3 58.7 %while.71 = (s32[]{:T(128)}, f32[3,256]{1,0:T(4,128)S(1)}, f32[3,256]{1,0:T(4,128)S(1)}, f32[3,256,1024]{2,1,0:T(8,128)S(1)}, f32[1024]{0:T(1024)S(1)}, /*index=...) while((s32[]{:T(128)}, f32[3,256]{1,0:T(4,128)S(1)}, ...), condition=%wide.region_9.10_spmd, body=%wide.region_4.9_spmd.sunk | while | flops 1358037248 | bytes 18910180 | solution.py:140
  221.8 10.9 %multiply_reduce_fusion.4 = f32[256]{0:T(256)S(1)} fusion(f32[3,256,2560]{2,1,0:T(8,128)} %get-tuple-element.835, s32[]{:T(128)S(6)} %select_n.124, f32[256]{0:T(256)S(1)} %get-tuple-element.751, f32[256]{0:T(256)S(1)} %multiply_add_fusion.9), kind=kLoop, calls=%fused_computation.30.clone.1 | loop fusion | flops 6553344 | bytes 2624516 | tf_op jit(solution)/shard_map/while/body/reduce_sum | solution.py:124
  232.7 13.3 %bitcast_dynamic-update-slice_fusion.4 = (f32[3,256,1024]{2,1,0:T(8,128)S(1)}, f32[256,1024]{1,0:T(8,128)S(1)}) fusion(f32[3,256,1024]{2,1,0:T(8,128)S(1)} %get-tuple-element.820, s32[]{:T(128)S(6)} %select_n.124, bf16[2560,1024]{1,0:T(8,128)(2,1)} %get-tuple-element.836, f32[256]{0:T(256)S(1)} %multiply_add_fusion.9, ...), kind=kOutput, calls=%fused_computation.35.clone.1 | convolution fusion | flops 1347420160 | bytes 9964544 | tf_op jit(solution)/shard_map/while/body/dot_general | solution.py:125
  250.9 10.9 %multiply_reduce_fusion.4 = f32[256]{0:T(256)S(1)} fusion(f32[3,256,2560]{2,1,0:T(8,128)} %get-tuple-element.835, s32[]{:T(128)S(6)} %select_n.124, f32[256]{0:T(256)S(1)} %get-tuple-element.751, f32[256]{0:T(256)S(1)} %multiply_add_fusion.9), kind=kLoop, calls=%fused_computation.30.clone.1 | loop fusion | flops 6553344 | bytes 2624516 | tf_op jit(solution)/shard_map/while/body/reduce_sum | solution.py:124
  261.9 13.3 %bitcast_dynamic-update-slice_fusion.4 = (f32[3,256,1024]{2,1,0:T(8,128)S(1)}, f32[256,1024]{1,0:T(8,128)S(1)}) fusion(f32[3,256,1024]{2,1,0:T(8,128)S(1)} %get-tuple-element.820, s32[]{:T(128)S(6)} %select_n.124, bf16[2560,1024]{1,0:T(8,128)(2,1)} %get-tuple-element.836, f32[256]{0:T(256)S(1)} %multiply_add_fusion.9, ...), kind=kOutput, calls=%fused_computation.35.clone.1 | convolution fusion | flops 1347420160 | bytes 9964544 | tf_op jit(solution)/shard_map/while/body/dot_general | solution.py:125
  276.0 73.4 %all-gather = f32[131072]{0:T(1024)} all-gather(f32[1024]{0:T(1024)S(1)} %get-tuple-element.348), channel_id=2, replica_groups=mesh['dp_0'=4,'dp_1'=4,'dp_2'=4,'dp_3'=2] {'dp_0','dp_1','dp_2','dp_3'}, dimensions={0}, use_global_device_ids=true | all-gather | bytes 528384 | tf_op jit(solution)/shard_map/all_gather | solution.py:27
  361.0 27.1 %while.72 = (s32[]{:T(128)}, f32[3,256,2560]{2,1,0:T(8,128)}, f32[3,256]{1,0:T(4,128)S(1)}, s32[]{:T(128)}, f32[3,256,1024]{2,1,0:T(8,128)S(1)}, /*index=5*/f32[...) while((s32[]{:T(128)}, f32[3,256,2560]{2,1,0:T(8,128)}, ...), condition=%wide.region_18.19_spmd, body=%wide.region_16.18_spmd.sunk | while | flops 1347026688 | bytes 38809828 | solution.py:160
  396.5 57.9 %while.73 = (s32[]{:T(128)}, f32[3,256]{1,0:T(4,128)S(1)}, f32[3,256]{1,0:T(4,128)S(1)}, f32[3,256,1024]{2,1,0:T(8,128)S(1)}, f32[1024]{0:T(1024)S(1)}, /*index=...) while((s32[]{:T(128)}, f32[3,256]{1,0:T(4,128)S(1)}, ...), condition=%wide.region_24.25_spmd, body=%wide.region_19.24_spmd.sunk | while | flops 1358037248 | bytes 18910180 | solution.py:140
  400.9 10.9 %multiply_reduce_fusion.5 = f32[256]{0:T(256)S(1)} fusion(f32[3,256,2560]{2,1,0:T(8,128)} %get-tuple-element.901, s32[]{:T(128)S(6)} %select_n.129, f32[256]{0:T(256)S(1)} %get-tuple-element.771, f32[256]{0:T(256)S(1)} %multiply_add_fusion.10), kind=kLoop, calls=%fused_computation.44.clone.1 | loop fusion | flops 6553344 | bytes 2624516 | tf_op jit(solution)/shard_map/while/body/reduce_sum | solution.py:124
  411.8 13.3 %bitcast_dynamic-update-slice_fusion.5 = (f32[3,256,1024]{2,1,0:T(8,128)S(1)}, f32[256,1024]{1,0:T(8,128)S(1)}) fusion(f32[3,256,1024]{2,1,0:T(8,128)S(1)} %get-tuple-element.886, s32[]{:T(128)S(6)} %select_n.129, bf16[2560,1024]{1,0:T(8,128)(2,1)} %get-tuple-element.902, f32[256]{0:T(256)S(1)} %multiply_add_fusion.10, ...), kind=kOutput, calls=%fused_computation.49.clone.1 | convolution fusion | flops 1347420160 | bytes 9964544 | tf_op jit(solution)/shard_map/while/body/dot_general | solution.py:125
  429.6 10.9 %multiply_reduce_fusion.5 = f32[256]{0:T(256)S(1)} fusion(f32[3,256,2560]{2,1,0:T(8,128)} %get-tuple-element.901, s32[]{:T(128)S(6)} %select_n.129, f32[256]{0:T(256)S(1)} %get-tuple-element.771, f32[256]{0:T(256)S(1)} %multiply_add_fusion.10), kind=kLoop, calls=%fused_computation.44.clone.1 | loop fusion | flops 6553344 | bytes 2624516 | tf_op jit(solution)/shard_map/while/body/reduce_sum | solution.py:124
  440.6 13.3 %bitcast_dynamic-update-slice_fusion.5 = (f32[3,256,1024]{2,1,0:T(8,128)S(1)}, f32[256,1024]{1,0:T(8,128)S(1)}) fusion(f32[3,256,1024]{2,1,0:T(8,128)S(1)} %get-tuple-element.886, s32[]{:T(128)S(6)} %select_n.129, bf16[2560,1024]{1,0:T(8,128)(2,1)} %get-tuple-element.902, f32[256]{0:T(256)S(1)} %multiply_add_fusion.10, ...), kind=kOutput, calls=%fused_computation.49.clone.1 | convolution fusion | flops 1347420160 | bytes 9964544 | tf_op jit(solution)/shard_map/while/body/dot_general | solution.py:125
  454.4 80.7 %all-gather.1 = f32[131072]{0:T(1024)} all-gather(f32[1024]{0:T(1024)S(1)} %get-tuple-element.351), channel_id=3, replica_groups=mesh['dp_0'=4,'dp_1'=4,'dp_2'=4,'dp_3'=2] {'dp_0','dp_1','dp_2','dp_3'}, dimensions={0}, use_global_device_ids=true | all-gather | bytes 528384 | tf_op jit(solution)/shard_map/all_gather | solution.py:27
  538.2 27.2 %while.74 = (s32[]{:T(128)}, f32[3,256,2560]{2,1,0:T(8,128)}, f32[3,256]{1,0:T(4,128)S(1)}, s32[]{:T(128)}, f32[3,256,1024]{2,1,0:T(8,128)S(1)}, /*index=5*/f32[...) while((s32[]{:T(128)}, f32[3,256,2560]{2,1,0:T(8,128)}, ...), condition=%wide.region_28.29_spmd, body=%wide.region_26.28_spmd.sunk | while | flops 1347026688 | bytes 38809828 | solution.py:160
  567.3 20.6 %psum.28 = f32[]{:T(128)} all-reduce(f32[]{:T(128)S(6)} %add.207), channel_id=1, replica_groups=mesh['dp_0'=4,'dp_1'=4,'dp_2'=4,'dp_3'=2] {'dp_0'}, use_global_device_ids=true, to_apply=%region_31.32 | all-reduce | flops 1 | bytes 8 | tf_op jit(solution)/shard_map/psum | solution.py:31
  588.6 10.3 %psum.29 = f32[]{:T(128)} all-reduce(f32[]{:T(128)} %psum.28), channel_id=1, replica_groups=mesh['dp_0'=4,'dp_1'=4,'dp_2'=4,'dp_3'=2] {'dp_1'}, use_global_device_ids=true, to_apply=%region_32.33 | all-reduce | flops 1 | bytes 8 | tf_op jit(solution)/shard_map/psum | solution.py:31
  (122 shorter events, 155.0 us)
Async XLA Ops:
  7.2 84.5 %all-gather.11.cloned.1.call-start = ((), (), s32[]{:S(2)}) async-start(), calls=%async_computation.2 | async-start | bytes 15851520 | tf_op jit(solution)/shard_map/all_gather | solution.py:77
  7.9 192.2 %all-gather.7.cloned.1.call-start = ((), (), s32[]{:S(2)}) async-start(), calls=%async_computation | async-start | bytes 10567680 | tf_op jit(solution)/shard_map/all_gather | solution.py:82
  109.7 62.2 %copy-start.6 = (s32[128]{0:T(128)S(1)}, s32[128]{0:T(128)}, u32[]{:S(2)}) copy-start(s32[128]{0:T(128)} %param.21) | copy-start | bytes 1540
  118.2 234.2 %all-gather.9.cloned.1.call-start = ((), (), s32[]{:S(2)}) async-start(), calls=%async_computation.1 | async-start | bytes 10567680 | tf_op jit(solution)/shard_map/all_gather | solution.py:83
  173.8 0.5 copy-start.2
  174.3 0.5 copy-start.4
  361.0 3.3 copy-start.1
  374.5 3.3 copy-start.1
  538.1 27.2 %copy-start.3 = (s32[3]{0:T(128)S(1)}, s32[3]{0:T(128)}, u32[]{:S(2)}) copy-start(s32[3]{0:T(128)} %copy-done.2) | copy-start | bytes 40
  538.1 27.2 %copy-start.5 = (pred[3]{0:T(512)(128)(4,1)S(1)}, pred[3]{0:T(512)(128)(4,1)}, u32[]{:S(2)}) copy-start(pred[3]{0:T(512)(128)(4,1)} %copy-done.4) | copy-start | bytes 13
  538.1 49.8 %copy-start.7 = (s32[128]{0:T(128)S(1)}, s32[128]{0:T(128)}, u32[]{:S(2)}) copy-start(s32[128]{0:T(128)} %param.21) | copy-start | bytes 1540
  538.2 3.3 copy-start
  551.7 3.3 copy-start
Sparse Core Ops, SparseCore 0:
  11.1 80.5 all-gather.10
  118.3 71.0 all-gather.6
  192.4 69.9 all-gather.8
where the time goes:
time: 635 us; the launch traced here: 626 us
  blocking collectives  250 us (39%)
  matrix products  106 us (17%)
  other arithmetic  90.9 us (14%)
  waiting for transfers between devices  81.9 us (13%)
  local copies, waits for them, and re-layouts  77 us (12%)
  between operations  18.6 us (3%)
    all_gather x2, blocking collectives, over_pieces(): return lax.all_gather(x, axis).max(0)  154 us
    all_gather x1, waiting for transfers between devices, per_device(): rotation_full = lax.all_gather(rotation, DP, axis=0, tiled=True)  81.2 us
    dot_general x4, matrix products, first_step(): jnp.dot(act_f.astype(jnp.bfloat16), value_q, preferred_element_type=jnp.f...  53.3 us
    pmax x4, blocking collectives, one_axis_at_a_time(): x = lax.pmax(x, axis)  52.3 us
    reduce_sum x4, other arithmetic, first_step(): act_err = jnp.sum((act_f - normed) * (act_f - normed), axis=1)  43.6 us
    psum x4, blocking collectives, over_axes(): return functools.reduce(lax.psum, axes, x)  43.6 us
    dot_general x4, matrix products, second_step(): jnp.dot(mix_f.astype(jnp.bfloat16), output_q, preferred_element_type=jnp....  24.8 us
    dot_general x2, matrix products, rotate_step(): jnp.dot(block_rows, rotation_full, preferred_element_type=jnp.float32)  21.2 us
  transfers between devices with their start and end apart: 3, of which 1 were waited for; matrix products, arithmetic and copies ran while one was open for 17% of the time, Pallas kernels for 0%

commit v1 on v0

v1 whole, which is shorter than its diff:
```python
import functools

import jax
import jax.numpy as jnp
from jax import lax
from jax.experimental import pallas as pl
from jax.experimental.pallas import tpu as pltpu
from jax.sharding import Mesh
from jax.sharding import PartitionSpec as P

DP = ("dp_0", "dp_1", "dp_2", "dp_3")
EPS_NORM = 1e-06
EPS_SCALE = 1e-06
CLIP_RATIO = 0.9
SOFT = (6.579714691285096, -12.986868668454669, 12.191614515303863, -6.570949514891455, 1.970640660123473)
ROW_STEP = 256
SUB = 16
LANES = 512
VMEM_LIMIT = 60 * 1024 * 1024


def soft_round(values):
    whole = jnp.round(values)
    rest = values - whole
    square = rest * rest
    poly = SOFT[4] * square + SOFT[3]
    for coefficient in (SOFT[2], SOFT[1], SOFT[0]):
        poly = poly * square + coefficient
    return whole + (rest * square) * poly


def fake_quant(values, step_size):
    return soft_round(jnp.clip(values / step_size, -8.0, 7.0)) * step_size


NEAR = [(dy, dc) for dy in range(4) for dc in range(2) if (dy, dc) != (0, 0)]
FAR = [(dx, dz) for dx in range(4) for dz in range(4) if (dx, dz) != (0, 0)]


def exchange_kernel(combine, x_ref, o_ref, near, mid, far, near_send, near_recv, far_send, far_recv):
    ix, iz, iy, ic = [lax.axis_index(name) for name in DP]
    near_ids = [{"dp_2": lax.rem(iy + dy, 4), "dp_3": lax.rem(ic + dc, 2)} for dy, dc in NEAR]
    far_ids = [{"dp_0": lax.rem(ix + dx, 4), "dp_1": lax.rem(iz + dz, 4)} for dx, dz in FAR]
    barrier = pltpu.get_barrier_semaphore()
    for peer in near_ids + far_ids:
        pl.semaphore_signal(barrier, inc=1, device_id=peer, device_id_type=pl.DeviceIdType.MESH)
    pl.semaphore_wait(barrier, len(NEAR) + len(FAR))

    def share(source, slots, me, ids, send, recv):
        copies = [
            pltpu.make_async_remote_copy(
                src_ref=source, dst_ref=slots.at[me], send_sem=send.at[k], recv_sem=recv.at[k],
                device_id=peer, device_id_type=pl.DeviceIdType.MESH,
            )
            for k, peer in enumerate(ids)
        ]
        for copy in copies:
            copy.start()
        slots[me] = source[...]
        for copy in copies:
            copy.wait()
        total = slots[0]
        for k in range(1, slots.shape[0]):
            total = combine(total, slots[k])
        return total

    mid[...] = share(x_ref, near, iy * 2 + ic, near_ids, near_send, near_recv)
    o_ref[...] = share(mid, far, ix * 4 + iz, far_ids, far_send, far_recv)


def exchange(combine, x, collective_id):
    shape = x.shape
    return pl.pallas_call(
        functools.partial(exchange_kernel, combine),
        out_shape=jax.ShapeDtypeStruct(shape, jnp.float32),
        in_specs=[pl.BlockSpec(memory_space=pltpu.VMEM)],
        out_specs=pl.BlockSpec(memory_space=pltpu.VMEM),
        scratch_shapes=[
            pltpu.VMEM((8,) + shape, jnp.float32),
            pltpu.VMEM(shape, jnp.float32),
            pltpu.VMEM((16,) + shape, jnp.float32),
            pltpu.SemaphoreType.DMA((len(NEAR),)),
            pltpu.SemaphoreType.DMA((len(NEAR),)),
            pltpu.SemaphoreType.DMA((len(FAR),)),
            pltpu.SemaphoreType.DMA((len(FAR),)),
        ],
        compiler_params=pltpu.CompilerParams(collective_id=collective_id, has_side_effects=True),
    )(x)


def quantize_rows(resid_ref, act_ref, square_ref, error_ref):
    width = resid_ref.shape[1]

    def step(index, carry):
        rows = pl.ds(pl.multiple_of(index * SUB, SUB), SUB)
        squares = jnp.zeros((SUB, 128), jnp.float32)
        tops = jnp.zeros((SUB, 128), jnp.float32)
        for start in range(0, width, 128):
            part = resid_ref[rows, start : start + 128]
            squares = squares + part * part
            tops = jnp.maximum(tops, jnp.abs(part))
        mean_sq = jnp.sum(squares, axis=1, keepdims=True) / width
        scale = lax.rsqrt(mean_sq + EPS_NORM)
        step_size = CLIP_RATIO * (jnp.max(tops, axis=1, keepdims=True) * scale) / 7.0 + EPS_SCALE
        gain = jnp.broadcast_to(scale / step_size, (SUB, 128))
        wide_step = jnp.broadcast_to(step_size, (SUB, 128))
        errors = jnp.zeros((SUB, 128), jnp.float32)
        for start in range(0, width, 128):
            units = resid_ref[rows, start : start + 128] * gain
            rounded = soft_round(jnp.minimum(jnp.maximum(units, -8.0), 7.0))
            gap = rounded - units
            errors = errors + gap * gap
            act_ref[rows, start : start + 128] = (rounded * wide_step).astype(jnp.bfloat16)
        square_ref[rows, :] = mean_sq
        error_ref[rows, :] = jnp.sum(errors, axis=1, keepdims=True) * (step_size * step_size)
        return carry

    lax.fori_loop(0, resid_ref.shape[0] // SUB, step, 0)


def quantize_mixed(mixed_ref, gain_ref, step_ref, mix_ref, error_ref):
    channels = mixed_ref.shape[1]

    def step(index, carry):
        rows = pl.ds(pl.multiple_of(index * SUB, SUB), SUB)
        errors = jnp.zeros((SUB, 128), jnp.float32)
        for start in range(0, channels, 128):
            cols = slice(start, start + 128)
            units = mixed_ref[rows, cols] * gain_ref[:, cols]
            rounded = soft_round(jnp.minimum(jnp.maximum(units, -8.0), 7.0))
            gap = (rounded - units) * step_ref[:, cols]
            errors = errors + gap * gap
            mix_ref[rows, cols] = (rounded * step_ref[:, cols]).astype(jnp.bfloat16)
        error_ref[rows, :] = jnp.sum(errors, axis=1, keepdims=True)
        return carry

    lax.fori_loop(0, mixed_ref.shape[0] // SUB, step, 0)


def live_column(len_ref, rows):
    first = pl.program_id(0) * rows
    return first + lax.broadcasted_iota(jnp.int32, (rows, 1), 0) < len_ref[0]


def mix_and_top(len_ref, act, vt_ref, mixed_ref, top_ref, top_buf):
    rows, channels = mixed_ref.shape
    mixed = lax.dot_general(
        act[...], vt_ref[0], (((1,), (1,)), ((), ())), preferred_element_type=jnp.float32
    )
    mixed_ref[...] = mixed
    live = live_column(len_ref, rows)
    tops = jnp.max(jnp.where(live, jnp.abs(mixed), 0.0).reshape(rows // 8, 8, channels), axis=0)

    @pl.when(pl.program_id(0) == 0)
    def _():
        top_buf[...] = tops

    @pl.when(pl.program_id(0) > 0)
    def _():
        top_buf[...] = jnp.maximum(top_buf[...], tops)

    @pl.when(pl.program_id(0) == pl.num_programs(0) - 1)
    def _():
        top_ref[...] = jnp.max(top_buf[...], axis=0, keepdims=True)


def first_kernel(len_ref, resid_ref, vt_ref, mixed_ref, square_ref, loss_ref, top_ref, act, err, top_buf):
    quantize_rows(resid_ref, act, square_ref, err)
    loss_ref[...] = square_ref[...] * err[...]
    mix_and_top(len_ref, act, vt_ref, mixed_ref, top_ref, top_buf)


def second_kernel(
    len_ref, resid_ref, mixed_ref, gain_ref, step_ref, square_ref, loss_ref, oq_ref, vt_ref,
    resid_out, mixed_out, square_out, loss_out, top_ref, mix, act, err, top_buf,
):
    quantize_mixed(mixed_ref, gain_ref, step_ref, mix, err)
    loss = loss_ref[...] + square_ref[...] * err[...]
    resid_out[...] = resid_ref[...] + jnp.dot(mix[...], oq_ref[0], preferred_element_type=jnp.float32)
    quantize_rows(resid_out, act, square_out, err)
    loss_out[...] = loss + square_out[...] * err[...]
    mix_and_top(len_ref, act, vt_ref, mixed_out, top_ref, top_buf)


def last_kernel(
    len_ref, resid_ref, mixed_ref, gain_ref, step_ref, square_ref, loss_ref, oq_ref, out_ref, sum_ref, mix, err
):
    quantize_mixed(mixed_ref, gain_ref, step_ref, mix, err)
    live = live_column(len_ref, out_ref.shape[0])
    loss = jnp.where(live, loss_ref[...] + square_ref[...] * err[...], 0.0)
    updated = resid_ref[...] + jnp.dot(mix[...], oq_ref[0], preferred_element_type=jnp.float32)
    out_ref[...] = jnp.where(live, updated, 0.0).astype(jnp.bfloat16)
    total = jnp.broadcast_to(jnp.sum(loss, axis=0, keepdims=True), sum_ref.shape)

    @pl.when(pl.program_id(0) == 0)
    def _():
        sum_ref[...] = total

    @pl.when(pl.program_id(0) > 0)
    def _():
        sum_ref[...] = sum_ref[...] + total


def row_spec(width):
    return pl.BlockSpec((ROW_STEP, width), lambda i: (i, 0))


def whole_spec(shape):
    return pl.BlockSpec(shape, lambda i: (0,) * len(shape))


def layer_spec(layer, rows, width):
    return pl.BlockSpec((1, rows, width), lambda i: (layer, 0, 0), pipeline_mode=pl.Buffered(1))


SCALAR = pl.BlockSpec(memory_space=pltpu.SMEM)


def f32(*shape):
    return jax.ShapeDtypeStruct(shape, jnp.float32)


def params():
    return pltpu.CompilerParams(vmem_limit_bytes=VMEM_LIMIT, dimension_semantics=("arbitrary",))


def first_pass(own_len, resid, value_all, layer):
    rows, width, channels = resid.shape[0], resid.shape[1], value_all.shape[1]
    return pl.pallas_call(
        first_kernel,
        grid=(rows // ROW_STEP,),
        in_specs=[SCALAR, row_spec(width), layer_spec(layer, channels, width)],
        out_specs=[row_spec(channels), row_spec(1), row_spec(1), whole_spec((1, channels))],
        out_shape=[f32(rows, channels), f32(rows, 1), f32(rows, 1), f32(1, channels)],
        scratch_shapes=[
            pltpu.VMEM((ROW_STEP, width), jnp.bfloat16),
            pltpu.VMEM((ROW_STEP, 1), jnp.float32),
            pltpu.VMEM((8, channels), jnp.float32),
        ],
        compiler_params=params(),
    )(own_len, resid, value_all)


def second_pass(own_len, resid, mixed, gain, step_size, square, loss, output_all, value_all, layer):
    rows, width, channels = resid.shape[0], resid.shape[1], value_all.shape[1]
    return pl.pallas_call(
        second_kernel,
        grid=(rows // ROW_STEP,),
        in_specs=[
            SCALAR, row_spec(width), row_spec(channels), whole_spec((1, channels)), whole_spec((1, channels)),
            row_spec(1), row_spec(1), layer_spec(layer, channels, width), layer_spec(layer + 1, channels, width),
        ],
        out_specs=[row_spec(width), row_spec(channels), row_spec(1), row_spec(1), whole_spec((1, channels))],
        out_shape=[f32(rows, width), f32(rows, channels), f32(rows, 1), f32(rows, 1), f32(1, channels)],
        scratch_shapes=[
            pltpu.VMEM((ROW_STEP, channels), jnp.bfloat16),
            pltpu.VMEM((ROW_STEP, width), jnp.bfloat16),
            pltpu.VMEM((ROW_STEP, 1), jnp.float32),
            pltpu.VMEM((8, channels), jnp.float32),
        ],
        compiler_params=params(),
    )(own_len, resid, mixed, gain, step_size, square, loss, output_all, value_all)


def last_pass(own_len, resid, mixed, gain, step_size, square, loss, output_all, layer):
    rows, width, channels = resid.shape[0], resid.shape[1], output_all.shape[1]
    return pl.pallas_call(
        last_kernel,
        grid=(rows // ROW_STEP,),
        in_specs=[
            SCALAR, row_spec(width), row_spec(channels), whole_spec((1, channels)), whole_spec((1, channels)),
            row_spec(1), row_spec(1), layer_spec(layer, channels, width),
        ],
        out_specs=[row_spec(width), whole_spec((1, 128))],
        out_shape=[jax.ShapeDtypeStruct((rows, width), jnp.bfloat16), f32(1, 128)],
        scratch_shapes=[
            pltpu.VMEM((ROW_STEP, channels), jnp.bfloat16),
            pltpu.VMEM((ROW_STEP, 1), jnp.float32),
        ],
        compiler_params=params(),
    )(own_len, resid, mixed, gain, step_size, square, loss, output_all)


def mix_scale(top):
    step_size = CLIP_RATIO * exchange(jnp.maximum, top, 1) / 7.0 + EPS_SCALE
    return 1.0 / step_size, step_size


def per_device(hidden, rotation, norm_gain, value_weight, output_weight, lengths):
    rows = hidden.shape[0]
    layers = norm_gain.shape[0]
    rotation_full = lax.all_gather(rotation, DP, axis=0, tiled=True)
    scaled = (norm_gain[:, :, None] * value_weight.astype(jnp.float32)).astype(jnp.bfloat16)
    left = jnp.concatenate(
        [hidden] + [jnp.transpose(scaled[l]) for l in range(layers)] + [output_weight[l] for l in range(layers)], axis=0
    )
    product = jnp.dot(left, rotation_full, preferred_element_type=jnp.float32)
    resid = product[:rows]
    part = value_weight.shape[2]
    value_t = product[rows : rows + layers * part].reshape(layers, part, -1)
    output = product[rows + layers * part :].reshape(layers, part, -1)
    value_tops = jnp.max(jnp.abs(value_t), axis=2, keepdims=True)
    value_q = fake_quant(value_t, value_tops / 7.0 + EPS_SCALE).astype(jnp.bfloat16)
    value_all = lax.all_gather(value_q, DP, axis=1, tiled=True)
    output_tops = exchange(jnp.maximum, jnp.max(jnp.abs(output), axis=1), 0)
    output_q = fake_quant(output, output_tops[:, None, :] / 7.0 + EPS_SCALE).astype(jnp.bfloat16)
    output_all = lax.all_gather(output_q, DP, axis=1, tiled=True)
    own_len = lax.dynamic_slice_in_dim(lengths, lax.axis_index(DP), 1)
    mixed, square, loss, top = first_pass(own_len, resid, value_all, 0)
    for layer in range(layers - 1):
        gain, step_size = mix_scale(top)
        resid, mixed, square, loss, top = second_pass(
            own_len, resid, mixed, gain, step_size, square, loss, output_all, value_all, layer
        )
    gain, step_size = mix_scale(top)
    out, local = last_pass(own_len, resid, mixed, gain, step_size, square, loss, output_all, layers - 1)
    total = exchange(jnp.add, local, 2)
    count = jnp.sum(lengths).astype(jnp.float32)
    return out, total[0, 0] / count


def solution(mesh):
    finer = Mesh(mesh.devices.reshape(4, 4, 4, 2), DP)
    in_specs = (P(DP, None), P(DP, None), P(), P(None, None, DP), P(None, DP, None), P())
    out_specs = (P(DP, None), P())
    return jax.shard_map(per_device, mesh=finer, in_specs=in_specs, out_specs=out_specs, check_vma=False)
```

time: 635 us -> 382 us (0.60); the launches traced: 626 us -> 381 us
  blocking collectives: 250 us -> 0 us
  Pallas kernels: 0 us -> 137 us
  matrix products: 106 us -> 15 us
  waiting for transfers between devices: 81.9 us -> 171 us
  other arithmetic: 90.9 us -> 6.83 us
  local copies, waits for them, and re-layouts: 77 us -> 34.6 us
    all_gather x2 -> x0, blocking collectives: 154 us -> none  [over_pieces(): return lax.all_gather(x, axis).max(0)]
    pallas_call x0 -> x7, Pallas kernels: none -> 137 us  [the longest x4 57.7 us: exchange(): pl.pallas_call(functools.partial(exchange_kernel, combine), out_shape=jax...]
    all_gather x2, waiting for transfers between devices: 0.02 us -> 92.9 us  [the longest x1 59.5 us: per_device(): value_all = lax.all_gather(value_q, DP, axis=1, tiled=True)]
    dot_general x11 -> x1, matrix products: 106 us -> 15 us  [per_device(): product = jnp.dot(left, rotation_full, preferred_element_type=jnp.float32)]
    reduce_sum x13 -> x0, other arithmetic: 68.7 us -> none  [the longest x4 43.6 us: first_step(): act_err = jnp.sum((act_f - normed) * (act_f - normed), axis=1)]
    pmax x4 -> x0, blocking collectives: 52.3 us -> none  [one_axis_at_a_time(): x = lax.pmax(x, axis)]
    psum x4 -> x0, blocking collectives: 43.6 us -> none  [over_axes(): return functools.reduce(lax.psum, axes, x)]
    while x10 -> x0, local copies, waits for them, and re-layouts: 20.7 us -> none  [the longest x2 15.9 us: per_device(): lax.fori_loop(0, own_blocks, first_step, first_init)]
  transfers between devices with their start and end apart: 3 -> 3, of which waited for: 1 -> 3; matrix products, arithmetic and copies ran while one was open for 17% -> 4% of each run, Pallas kernels for 0% -> 10%
where the time goes in v1:
time: 382 us; the launch traced here: 381 us
  waiting for transfers between devices  171 us (45%)
  Pallas kernels  137 us (36%)
  local copies, waits for them, and re-layouts  34.6 us (9%)
  between operations  16.3 us (4%)
  matrix products  15 us (4%)
  other arithmetic  6.83 us (2%)
    all_gather x1, waiting for transfers between devices, per_device(): rotation_full = lax.all_gather(rotation, DP, axis=0, tiled=True)  76.9 us
    all_gather x1, waiting for transfers between devices, per_device(): value_all = lax.all_gather(value_q, DP, axis=1, tiled=True)  59.5 us
    pallas_call x4, Pallas kernels, exchange(): pl.pallas_call(functools.partial(exchange_kernel, combine), out_shape=jax...  57.7 us
    pallas_call x1, Pallas kernels, second_pass(): pl.pallas_call(second_kernel, grid=(rows // ROW_STEP,), in_specs=[SCALAR,...  38.4 us
    all_gather x1, waiting for transfers between devices, per_device(): output_all = lax.all_gather(output_q, DP, axis=1, tiled=True)  33.4 us
    unnamed x15, local copies, waits for them, and re-layouts  26.5 us
    pallas_call x1, Pallas kernels, first_pass(): pl.pallas_call(first_kernel, grid=(rows // ROW_STEP,), in_specs=[SCALAR,...  24.5 us
    pallas_call x1, Pallas kernels, last_pass(): pl.pallas_call(last_kernel, grid=(rows // ROW_STEP,), in_specs=[SCALAR, r...  16.5 us
  transfers between devices with their start and end apart: 3, of which 3 were waited for; matrix products, arithmetic and copies ran while one was open for 4% of the time, Pallas kernels for 10%

profile of v1, /device:TPU:0, one launch (start us, length us, event | category | flops | bytes accessed | tf_op | source)
XLA Modules:
  0.0 381.2 jit_solution(10748559552183961411)
XLA Ops:
  7.2 0.7 all-gather.9.cloned.1.call-update
  8.0 4.3 %constant_dynamic-update-slice_fusion = bf16[800,2560]{1,0:T(8,128)(2,1)} fusion(bf16[768,2560]{1,0:T(8,128)(2,1)} %param.6), kind=kLoop, calls=%fused_computation.41 | loop fusion | bytes 7864320
  12.9 0.6 fusion.15
  13.5 0.6 bitcast_dynamic-update-slice_fusion.1
  14.7 76.9 %all-gather.9.cloned.1.call-done = bf16[128,20,2560]{2,1,0:T(8,128)(2,1)} async-done(((bf16[1,20,2560]{2,1,0:T(8,128)(2,1)}), bf16[128,20,2560]{2,1,0:T(8,128)(2,1)}) %all-gather.9.cloned.1.call-update) | async-done | bytes 13107216 | tf_op jit(solution)/shard_map/all_gather | solution.py:292
  91.7 17.9 %reshape.31 = bf16[2560,2560]{1,0:T(8,128)(2,1)} reshape(bf16[128,20,2560]{2,1,0:T(8,128)(2,1)} %all-gather.9.cloned.1.call-done) | data formatting | bytes 26214400
  109.6 15.0 %fusion.17 = f32[800,2560]{1,0:T(8,128)S(1)} fusion(bf16[800,2560]{1,0:T(8,128)(2,1)} %bitcast_dynamic-update-slice_fusion, bf16[2560,2560]{1,0:T(8,128)(2,1)} %reshape.31), kind=kOutput, calls=%fused_computation.47 | convolution fusion | flops 10485760000 | bytes 25395200 | tf_op jit(solution)/shard_map/dot_general | solution.py:297
  124.6 0.8 abs_reduce_fusion.x_ref
  125.4 2.4 copy-done
  127.9 18.1 %shard_map.79 = f32[2,2560]{1,0:T(2,128)} custom-call(f32[2,2560]{1,0:T(2,128)} %abs_reduce_fusion.x_ref), custom_call_target="tpu_custom_call" | custom-call | tf_op jit(solution)/shard_map/pallas_call | solution.py:73
  146.0 0.7 multiply_add_fusion
  146.8 1.9 fusion.13
  149.5 0.7 reduce_sum.9
  151.4 6.9 %slice.34.resid_ref = f32[768,2560]{1,0:T(8,128)} slice(f32[800,2560]{1,0:T(8,128)} %copy-done), slice={[0:768], [0:2560]} | slice | bytes 15728640 | tf_op jit(solution)/shard_map/slice | solution.py:298
  158.3 59.5 %all-gather.5.cloned.1.call-done.vt_ref = bf16[2,1024,2560]{2,1,0:T(8,128)(2,1)} async-done(((bf16[2,8,2560]{2,1,0:T(8,128)(2,1)}), bf16[2,1024,2560]{2,1,0:T(8,128)(2,1)}) %all-gather.5.cloned.1.call-update) | async-done | bytes 10485776 | tf_op jit(solution)/shard_map/all_gather | solution.py:304
  217.8 24.5 %shard_map.77 = (f32[768,1024]{1,0:T(8,128)}, f32[768,1]{1,0:T(8,128)}, f32[768,1]{1,0:T(8,128)}, f32[1,1024]{1,0:T(1,128)}) custom-call(s32[1]{0:T(128)} %dynamic_slice.3.len_ref, f32[768,2560]{1,0:T(8,128)} %slice.34.resid_ref, bf16[2,1024,2560]{2,1,0:T(8,128)(2,1)} %all-gather.5.cloned.1.call-done.vt_ref), custom_call_target="tpu_custom_call" | custom-call | tf_op jit(solution)/shard_map/pallas_call | solution.py:229
  242.3 13.9 %shard_map.78 = f32[1,1024]{1,0:T(1,128)} custom-call(f32[1,1024]{1,0:T(1,128)} %get-tuple-element.14.x_ref), custom_call_target="tpu_custom_call" | custom-call | tf_op jit(solution)/shard_map/pallas_call | solution.py:73
  256.2 1.3 multiply_add_fusion.2
  257.5 33.4 %all-gather.7.cloned.1.call-done.oq_ref = bf16[2,1024,2560]{2,1,0:T(8,128)(2,1)} async-done(((bf16[2,8,2560]{2,1,0:T(8,128)(2,1)}), bf16[2,1024,2560]{2,1,0:T(8,128)(2,1)}) %all-gather.7.cloned.1.call-update) | async-done | bytes 10485776 | tf_op jit(solution)/shard_map/all_gather | solution.py:307
  290.9 38.4 %shard_map.80 = (f32[768,2560]{1,0:T(8,128)}, f32[768,1024]{1,0:T(8,128)}, f32[768,1]{1,0:T(8,128)}, f32[768,1]{1,0:T(8,128)}, f32[1,1024]{1,0:T(1,128)}) custom-call(s32[1]{0:T(128)} %dynamic_slice.3.len_ref, f32[768,2560]{1,0:T(8,128)} %slice.34.resid_ref, f32[768,1024]{1,0:T(8,128)} %get-tuple-element.13.mixed_ref, f32[1,1024]{1,0:T(1,128)} %get-tuple-element.29.gain_ref, ...), custom_call_target="tpu_custom_call" | custom-call | tf_op jit(solution)/shard_map/pallas_call | solution.py:246
  329.4 13.9 %shard_map.81 = f32[1,1024]{1,0:T(1,128)} custom-call(f32[1,1024]{1,0:T(1,128)} %get-tuple-element.19.x_ref), custom_call_target="tpu_custom_call" | custom-call | tf_op jit(solution)/shard_map/pallas_call | solution.py:73
  343.3 1.3 multiply_add_fusion.1
  344.6 16.5 %shard_map.82 = (bf16[768,2560]{1,0:T(8,128)(2,1)}, f32[1,128]{1,0:T(1,128)}) custom-call(s32[1]{0:T(128)} %dynamic_slice.3.len_ref, f32[768,2560]{1,0:T(8,128)} %get-tuple-element.17.resid_ref, f32[768,1024]{1,0:T(8,128)} %get-tuple-element.18.mixed_ref, f32[1,1024]{1,0:T(1,128)} %get-tuple-element.27.gain_ref, f32[1,1024]{1,0:T(1,128)} %get-tuple-element.26.step_ref, ...), custom_call_target="tpu_custom_call" | custom-call | tf_op jit(solution)/shard_map/pallas_call | solution.py:267
  361.1 11.9 %shard_map.83 = f32[1,128]{1,0:T(1,128)} custom-call(f32[1,128]{1,0:T(1,128)} %get-tuple-element.23.x_ref), custom_call_target="tpu_custom_call" | custom-call | tf_op jit(solution)/shard_map/pallas_call | solution.py:73
  (21 shorter events, 2.9 us)
Async XLA Ops:
  7.2 5.1 %copy-start.3 = (f32[2,2560]{1,0:T(2,128)S(1)}, f32[2,2560]{1,0:T(2,128)}, u32[]{:S(2)}) copy-start(f32[2,2560]{1,0:T(2,128)} %param.8) | copy-start | bytes 61444
  7.2 5.1 %copy-start.1 = (bf16[2,2560,8]{1,2,0:T(8,128)(2,1)S(1)}, bf16[2,2560,8]{1,2,0:T(8,128)(2,1)}, u32[]{:S(2)}) copy-start(bf16[2,2560,8]{1,2,0:T(8,128)(2,1)} %param.9) | copy-start | bytes 245764
  7.2 84.5 %all-gather.9.cloned.1.call-start = ((), (), s32[]{:S(2)}) async-start(), calls=%async_computation.2 | async-start | bytes 15851520 | tf_op jit(solution)/shard_map/all_gather | solution.py:292
  7.9 5.6 %copy-start.2 = (bf16[2,8,2560]{2,1,0:T(8,128)(2,1)S(1)}, bf16[2,8,2560]{2,1,0:T(8,128)(2,1)}, u32[]{:S(2)}) copy-start(bf16[2,8,2560]{2,1,0:T(8,128)(2,1)} %param.10) | copy-start | bytes 245764
  7.9 209.9 %all-gather.5.cloned.1.call-start = ((), (), s32[]{:S(2)}) async-start(), calls=%async_computation | async-start | bytes 10567680 | tf_op jit(solution)/shard_map/all_gather | solution.py:304
  109.6 39.9 %copy-start.4 = (s32[128]{0:T(128)S(1)}, s32[128]{0:T(128)}, u32[]{:S(2)}) copy-start(s32[128]{0:T(128)} %param.11) | copy-start | bytes 1540
  124.6 3.2 copy-start
  148.7 142.2 %all-gather.7.cloned.1.call-start = ((), (), s32[]{:S(2)}) async-start(), calls=%async_computation.1 | async-start | bytes 10567680 | tf_op jit(solution)/shard_map/all_gather | solution.py:307
Sparse Core Ops, SparseCore 0:
  11.1 80.5 all-gather.8
  148.8 68.9 all-gather.4
  220.8 70.0 all-gather.6

commit v2 on v1

--- a/solution.py
+++ b/solution.py
@@ -17,6 +17,7 @@
 SUB = 16
 LANES = 512
 VMEM_LIMIT = 60 * 1024 * 1024
+MESH_ID = pl.DeviceIdType.MESH
 
 
 def soft_round(values):
@@ -86,6 +87,263 @@
         ],
         compiler_params=pltpu.CompilerParams(collective_id=collective_id, has_side_effects=True),
     )(x)
+
+
+RING = 4
+COLORS = ((0, 1, 2), (1, 2, 0), (2, 0, 1))
+PER_COLOR = 24
+
+
+def places():
+    return [lax.axis_index(name) for name in DP]
+
+
+def neighbours(place):
+    ids = []
+    for axis in range(3):
+        for shift in (1, RING - 1):
+            ids.append({DP[axis]: lax.rem(place[axis] + shift, RING)})
+    ids.append({DP[3]: 1 - place[3]})
+    return ids
+
+
+def greet(place):
+    barrier = pltpu.get_barrier_semaphore()
+    ids = neighbours(place)
+    for peer in ids:
+        pl.semaphore_signal(barrier, inc=1, device_id=peer, device_id_type=MESH_ID)
+    return lambda: pl.semaphore_wait(barrier, len(ids))
+
+
+class Gather:
+    def __init__(self, buffer, place, send, recv, first_row, rows, first_column, widths):
+        self.buffer, self.place, self.send, self.recv = buffer, place, send, recv
+        self.half = buffer.shape[4] // 2
+        self.first_row, self.rows = first_row, rows
+        self.first_column, self.widths = first_column, widths
+        self.partner = {DP[3]: 1 - place[3]}
+        self.pending = []
+        self.counter = 0
+
+    def view(self, color, position, axis, done, part=None):
+        start = self.first_column + sum(self.widths[:color])
+        cols = pl.ds(pl.multiple_of(self.place[3] * self.half + start, 128), self.widths[color])
+        index = [self.place[k] for k in range(3)]
+        for k in done:
+            index[k] = slice(None)
+        index[axis] = position
+        rows = pl.ds(self.first_row, self.rows)
+        if part is not None:
+            if done:
+                index[done[0]] = pl.ds(2 * part, 2)
+            else:
+                cut = (self.rows // 2 + 7) // 8 * 8
+                rows = pl.ds(self.first_row, cut) if part == 0 else pl.ds(self.first_row + cut, self.rows - cut)
+        return self.buffer.at[index[0], index[1], index[2], rows, cols]
+
+    def copy(self, view, peer):
+        slot = self.counter
+        self.counter += 1
+        copy = pltpu.make_async_remote_copy(
+            src_ref=view, dst_ref=view, send_sem=self.send.at[slot], recv_sem=self.recv.at[slot],
+            device_id=peer, device_id_type=MESH_ID,
+        )
+        copy.start()
+        self.pending.append((copy, peer is self.partner))
+        return copy
+
+    def steps(self):
+        state = {}
+
+        def begin(phase):
+            for color, order in enumerate(COLORS):
+                axis, done = order[phase], order[:phase]
+                own = self.place[axis]
+                up = {DP[axis]: lax.rem(own + 1, RING)}
+                down = {DP[axis]: lax.rem(own + RING - 1, RING)}
+                block = self.view(color, own, axis, done)
+                state[phase, color] = [self.copy(block, up), self.copy(block, down)]
+
+        def relay(phase):
+            for color, order in enumerate(COLORS):
+                axis, done = order[phase], order[:phase]
+                own = self.place[axis]
+                above, below = lax.rem(own + 1, RING), lax.rem(own + RING - 1, RING)
+                from_below, from_above = state[phase, color]
+                from_below.wait_recv()
+                first = self.copy(self.view(color, below, axis, done, 0), {DP[axis]: above})
+                self.copy(self.view(color, below, axis, done), self.partner)
+                from_above.wait_recv()
+                second = self.copy(self.view(color, above, axis, done, 1), {DP[axis]: below})
+                self.copy(self.view(color, above, axis, done), self.partner)
+                state[phase, color] = [first, second]
+
+        def finish(phase):
+            for color, order in enumerate(COLORS):
+                axis, done = order[phase], order[:phase]
+                across = lax.rem(self.place[axis] + 2, RING)
+                for copy in state[phase, color]:
+                    copy.wait_recv()
+                self.copy(self.view(color, across, axis, done), self.partner)
+
+        result = []
+        for phase in range(3):
+            if phase == 0:
+                result.append(lambda: begin(0))
+            result.append(functools.partial(relay, phase))
+            if phase < 2:
+                def turn(phase=phase):
+                    finish(phase)
+                    begin(phase + 1)
+                result.append(turn)
+            else:
+                result.append(functools.partial(finish, phase))
+        result.append(self.drain)
+        return result
+
+    def drain(self):
+        for copy, kept in self.pending:
+            copy.wait_send()
+            if kept:
+                copy.wait_recv()
+
+
+def rotate_kernel(rotation_ref, hidden_ref, weight_ref, product_ref, full, left, pair, wide, send, recv, pair_send, pair_recv, local):
+    place = places()
+    ready = greet(place)
+    rows = rotation_ref.shape[0]
+    tokens = hidden_ref.shape[0]
+    loads = [
+        pltpu.make_async_copy(hidden_ref, left.at[pl.ds(0, tokens)], local.at[0]),
+        pltpu.make_async_copy(weight_ref, left.at[pl.ds(tokens, weight_ref.shape[0])], local.at[1]),
+    ]
+    for load in loads:
+        load.start()
+    core = place[3]
+    ready()
+    swap = pltpu.make_async_remote_copy(
+        src_ref=rotation_ref, dst_ref=pair.at[core], send_sem=pair_send, recv_sem=pair_recv,
+        device_id={DP[3]: 1 - core}, device_id_type=MESH_ID,
+    )
+    swap.start()
+    pair[core] = rotation_ref[...]
+    swap.wait()
+    for k in range(2):
+        wide[k * rows : (k + 1) * rows, :] = pair[k].astype(jnp.float32)
+    full[place[0], place[1], place[2]] = wide[...].astype(jnp.bfloat16)
+    early = Gather(full, place, send.at[0], recv.at[0], 0, 2 * rows, 0, (256, 256, 256))
+    late = Gather(full, place, send.at[1], recv.at[1], 0, 2 * rows, 768, (256, 128, 128))
+    one, two = early.steps(), late.steps()
+    for k in range(4):
+        one[k]()
+        two[k]()
+    one[4]()
+    one[5]()
+    two[4]()
+    for load in loads:
+        load.wait()
+    depth = left.shape[1]
+    width = 256
+
+    def columns(first, count):
+        def body(index, carry):
+            for core_half in range(2):
+                cols = pl.ds(pl.multiple_of(core_half * (depth // 2) + first + index * width, width), width)
+                block = full[:, :, :, :, cols].reshape(depth, width)
+                product_ref[:, cols] = jnp.dot(left[...], block, preferred_element_type=jnp.float32)
+            return carry
+
+        lax.fori_loop(0, count, body, 0)
+
+    one[6]()
+    one[7]()
+    columns(0, 2)
+    two[5]()
+    columns(512, 1)
+    two[6]()
+    two[7]()
+    columns(768, 2)
+
+
+def rotate(rotation, hidden, weights):
+    rows, depth = rotation.shape
+    total = hidden.shape[0] + weights.shape[0]
+    return pl.pallas_call(
+        rotate_kernel,
+        out_shape=jax.ShapeDtypeStruct((total, depth), jnp.float32),
+        in_specs=[
+            pl.BlockSpec(memory_space=pltpu.VMEM),
+            pl.BlockSpec(memory_space=pl.ANY),
+            pl.BlockSpec(memory_space=pl.ANY),
+        ],
+        out_specs=pl.BlockSpec(memory_space=pltpu.VMEM),
+        scratch_shapes=[
+            pltpu.VMEM((RING, RING, RING, 2 * rows, depth), jnp.bfloat16),
+            pltpu.VMEM((total, depth), jnp.bfloat16),
+            pltpu.VMEM((2, rows, depth), jnp.bfloat16),
+            pltpu.VMEM((2 * rows, depth), jnp.float32),
+            pltpu.SemaphoreType.DMA((2, 63)),
+            pltpu.SemaphoreType.DMA((2, 63)),
+            pltpu.SemaphoreType.DMA,
+            pltpu.SemaphoreType.DMA,
+            pltpu.SemaphoreType.DMA((2,)),
+        ],
+        compiler_params=pltpu.CompilerParams(
+            collective_id=3, has_side_effects=True, vmem_limit_bytes=VMEM_LIMIT
+        ),
+    )(rotation, hidden, weights)
+
+
+def spread_kernel(shard_ref, full, send, recv, swap_send, swap_recv, local):
+    place = places()
+    ready = greet(place)
+    count, rows = shard_ref.shape[0], shard_ref.shape[1]
+    core = place[3]
+    spots = [
+        full.at[place[0], place[1], place[2], pl.ds(pl.multiple_of(2 * rows * k + rows * core, rows), rows)]
+        for k in range(count)
+    ]
+    loads = [pltpu.make_async_copy(shard_ref.at[k], spots[k], local.at[k]) for k in range(count)]
+    for load in loads:
+        load.start()
+    ready()
+    swaps = []
+    for k in range(count):
+        loads[k].wait()
+        swap = pltpu.make_async_remote_copy(
+            src_ref=spots[k], dst_ref=spots[k], send_sem=swap_send.at[k], recv_sem=swap_recv.at[k],
+            device_id={DP[3]: 1 - core}, device_id_type=MESH_ID,
+        )
+        swap.start()
+        swaps.append(swap)
+    for swap in swaps:
+        swap.wait()
+    half = count * rows
+    early = Gather(full, place, send.at[0], recv.at[0], 0, half, 0, (512, 384, 384))
+    late = Gather(full, place, send.at[1], recv.at[1], half, half, 0, (384, 512, 384))
+    for first, second in zip(early.steps(), late.steps()):
+        first()
+        second()
+
+
+def spread(shard):
+    count, rows, depth = shard.shape
+    return pl.pallas_call(
+        spread_kernel,
+        out_shape=jax.ShapeDtypeStruct((RING, RING, RING, 2 * rows * count, depth), jnp.bfloat16),
+        in_specs=[pl.BlockSpec(memory_space=pl.ANY)],
+        out_specs=pl.BlockSpec(memory_space=pltpu.VMEM),
+        scratch_shapes=[
+            pltpu.SemaphoreType.DMA((2, 63)),
+            pltpu.SemaphoreType.DMA((2, 63)),
+            pltpu.SemaphoreType.DMA((count,)),
+            pltpu.SemaphoreType.DMA((count,)),
+            pltpu.SemaphoreType.DMA((count,)),
+        ],
+        compiler_params=pltpu.CompilerParams(
+            collective_id=4, has_side_effects=True, vmem_limit_bytes=VMEM_LIMIT
+        ),
+    )(shard)
 
 
 def quantize_rows(resid_ref, act_ref, square_ref, error_ref):
@@ -145,7 +403,7 @@
 def mix_and_top(len_ref, act, vt_ref, mixed_ref, top_ref, top_buf):
     rows, channels = mixed_ref.shape
     mixed = lax.dot_general(
-        act[...], vt_ref[0], (((1,), (1,)), ((), ())), preferred_element_type=jnp.float32
+        act[...], vt_ref[...].reshape(channels, act.shape[1]), (((1,), (1,)), ((), ())), preferred_element_type=jnp.float32
     )
     mixed_ref[...] = mixed
     live = live_column(len_ref, rows)
@@ -176,7 +434,7 @@
 ):
     quantize_mixed(mixed_ref, gain_ref, step_ref, mix, err)
     loss = loss_ref[...] + square_ref[...] * err[...]
-    resid_out[...] = resid_ref[...] + jnp.dot(mix[...], oq_ref[0], preferred_element_type=jnp.float32)
+    resid_out[...] = resid_ref[...] + jnp.dot(mix[...], oq_ref[...].reshape(mix.shape[1], oq_ref.shape[2]), preferred_element_type=jnp.float32)
     quantize_rows(resid_out, act, square_out, err)
     loss_out[...] = loss + square_out[...] * err[...]
     mix_and_top(len_ref, act, vt_ref, mixed_out, top_ref, top_buf)
@@ -188,7 +446,7 @@
     quantize_mixed(mixed_ref, gain_ref, step_ref, mix, err)
     live = live_column(len_ref, out_ref.shape[0])
     loss = jnp.where(live, loss_ref[...] + square_ref[...] * err[...], 0.0)
-    updated = resid_ref[...] + jnp.dot(mix[...], oq_ref[0], preferred_element_type=jnp.float32)
+    updated = resid_ref[...] + jnp.dot(mix[...], oq_ref[...].reshape(mix.shape[1], oq_ref.shape[2]), preferred_element_type=jnp.float32)
     out_ref[...] = jnp.where(live, updated, 0.0).astype(jnp.bfloat16)
     total = jnp.broadcast_to(jnp.sum(loss, axis=0, keepdims=True), sum_ref.shape)
 
@@ -209,8 +467,8 @@
     return pl.BlockSpec(shape, lambda i: (0,) * len(shape))
 
 
-def layer_spec(layer, rows, width):
-    return pl.BlockSpec((1, rows, width), lambda i: (layer, 0, 0), pipeline_mode=pl.Buffered(1))
+def layer_spec(which, rows, width):
+    return pl.BlockSpec((rows // 16, 16, width), lambda i: (0, which, 0), pipeline_mode=pl.Buffered(1))
 
 
 SCALAR = pl.BlockSpec(memory_space=pltpu.SMEM)
@@ -224,12 +482,12 @@
     return pltpu.CompilerParams(vmem_limit_bytes=VMEM_LIMIT, dimension_semantics=("arbitrary",))
 
 
-def first_pass(own_len, resid, value_all, layer):
-    rows, width, channels = resid.shape[0], resid.shape[1], value_all.shape[1]
+def first_pass(own_len, rows, resid, weights, layer):
+    width, channels = resid.shape[1], weights.shape[0] * 16
     return pl.pallas_call(
         first_kernel,
         grid=(rows // ROW_STEP,),
-        in_specs=[SCALAR, row_spec(width), layer_spec(layer, channels, width)],
+        in_specs=[SCALAR, row_spec(width), layer_spec(2 * layer, channels, width)],
         out_specs=[row_spec(channels), row_spec(1), row_spec(1), whole_spec((1, channels))],
         out_shape=[f32(rows, channels), f32(rows, 1), f32(rows, 1), f32(1, channels)],
         scratch_shapes=[
@@ -238,17 +496,17 @@
             pltpu.VMEM((8, channels), jnp.float32),
         ],
         compiler_params=params(),
-    )(own_len, resid, value_all)
-
-
-def second_pass(own_len, resid, mixed, gain, step_size, square, loss, output_all, value_all, layer):
-    rows, width, channels = resid.shape[0], resid.shape[1], value_all.shape[1]
+    )(own_len, resid, weights)
+
+
+def second_pass(own_len, rows, resid, mixed, gain, step_size, square, loss, weights, layer):
+    width, channels = resid.shape[1], mixed.shape[1]
     return pl.pallas_call(
         second_kernel,
         grid=(rows // ROW_STEP,),
         in_specs=[
             SCALAR, row_spec(width), row_spec(channels), whole_spec((1, channels)), whole_spec((1, channels)),
-            row_spec(1), row_spec(1), layer_spec(layer, channels, width), layer_spec(layer + 1, channels, width),
+            row_spec(1), row_spec(1), layer_spec(2 * layer + 1, channels, width), layer_spec(2 * layer + 2, channels, width),
         ],
         out_specs=[row_spec(width), row_spec(channels), row_spec(1), row_spec(1), whole_spec((1, channels))],
         out_shape=[f32(rows, width), f32(rows, channels), f32(rows, 1), f32(rows, 1), f32(1, channels)],
@@ -259,17 +517,17 @@
             pltpu.VMEM((8, channels), jnp.float32),
         ],
         compiler_params=params(),
-    )(own_len, resid, mixed, gain, step_size, square, loss, output_all, value_all)
-
-
-def last_pass(own_len, resid, mixed, gain, step_size, square, loss, output_all, layer):
-    rows, width, channels = resid.shape[0], resid.shape[1], output_all.shape[1]
+    )(own_len, resid, mixed, gain, step_size, square, loss, weights, weights)
+
+
+def last_pass(own_len, rows, resid, mixed, gain, step_size, square, loss, weights, layer):
+    width, channels = resid.shape[1], mixed.shape[1]
     return pl.pallas_call(
         last_kernel,
         grid=(rows // ROW_STEP,),
         in_specs=[
             SCALAR, row_spec(width), row_spec(channels), whole_spec((1, channels)), whole_spec((1, channels)),
-            row_spec(1), row_spec(1), layer_spec(layer, channels, width),
+            row_spec(1), row_spec(1), layer_spec(2 * layer + 1, channels, width),
         ],
         out_specs=[row_spec(width), whole_spec((1, 128))],
         out_shape=[jax.ShapeDtypeStruct((rows, width), jnp.bfloat16), f32(1, 128)],
@@ -278,7 +536,7 @@
             pltpu.VMEM((ROW_STEP, 1), jnp.float32),
         ],
         compiler_params=params(),
-    )(own_len, resid, mixed, gain, step_size, square, loss, output_all)
+    )(own_len, resid, mixed, gain, step_size, square, loss, weights)
 
 
 def mix_scale(top):
@@ -287,33 +545,29 @@
 
 
 def per_device(hidden, rotation, norm_gain, value_weight, output_weight, lengths):
-    rows = hidden.shape[0]
-    layers = norm_gain.shape[0]
-    rotation_full = lax.all_gather(rotation, DP, axis=0, tiled=True)
+    rows, width = hidden.shape
+    layers, part = output_weight.shape[0], output_weight.shape[1]
     scaled = (norm_gain[:, :, None] * value_weight.astype(jnp.float32)).astype(jnp.bfloat16)
-    left = jnp.concatenate(
-        [hidden] + [jnp.transpose(scaled[l]) for l in range(layers)] + [output_weight[l] for l in range(layers)], axis=0
-    )
-    product = jnp.dot(left, rotation_full, preferred_element_type=jnp.float32)
-    resid = product[:rows]
-    part = value_weight.shape[2]
-    value_t = product[rows : rows + layers * part].reshape(layers, part, -1)
-    output = product[rows + layers * part :].reshape(layers, part, -1)
+    own = jnp.stack([jnp.transpose(scaled, (0, 2, 1)), output_weight], axis=1)
+    product = rotate(rotation, hidden, own.reshape(2 * layers * part, width))
+    turned = product[rows:].reshape(layers, 2, part, width)
+    value_t, output = turned[:, 0], turned[:, 1]
+    output_tops = exchange(jnp.maximum, jnp.max(jnp.abs(output), axis=1), 0)
     value_tops = jnp.max(jnp.abs(value_t), axis=2, keepdims=True)
-    value_q = fake_quant(value_t, value_tops / 7.0 + EPS_SCALE).astype(jnp.bfloat16)
-    value_all = lax.all_gather(value_q, DP, axis=1, tiled=True)
-    output_tops = exchange(jnp.maximum, jnp.max(jnp.abs(output), axis=1), 0)
-    output_q = fake_quant(output, output_tops[:, None, :] / 7.0 + EPS_SCALE).astype(jnp.bfloat16)
-    output_all = lax.all_gather(output_q, DP, axis=1, tiled=True)
+    value_q = fake_quant(value_t, value_tops / 7.0 + EPS_SCALE)
+    output_q = fake_quant(output, output_tops[:, None, :] / 7.0 + EPS_SCALE)
+    shard = jnp.stack([value_q, output_q], axis=1).astype(jnp.bfloat16).reshape(2 * layers, part, width)
+    weights = spread(shard).reshape(RING**3, 4 * layers * part, width)
     own_len = lax.dynamic_slice_in_dim(lengths, lax.axis_index(DP), 1)
-    mixed, square, loss, top = first_pass(own_len, resid, value_all, 0)
+    resid = product
+    mixed, square, loss, top = first_pass(own_len, rows, resid, weights, 0)
     for layer in range(layers - 1):
         gain, step_size = mix_scale(top)
         resid, mixed, square, loss, top = second_pass(
-            own_len, resid, mixed, gain, step_size, square, loss, output_all, value_all, layer
+            own_len, rows, resid, mixed, gain, step_size, square, loss, weights, layer
         )
     gain, step_size = mix_scale(top)
-    out, local = last_pass(own_len, resid, mixed, gain, step_size, square, loss, output_all, layers - 1)
+    out, local = last_pass(own_len, rows, resid, mixed, gain, step_size, square, loss, weights, layers - 1)
     total = exchange(jnp.add, local, 2)
     count = jnp.sum(lengths).astype(jnp.float32)
     return out, total[0, 0] / count

time: 382 us -> 272 us (0.71)
  waiting for transfers between devices: 171 us -> 0 us
  Pallas kernels: 137 us -> 258 us
  local copies, waits for them, and re-layouts: 34.6 us -> 2.92 us
  matrix products: 15 us -> 0 us
  between operations: 16.3 us -> 3.2 us
    all_gather x3 -> x0, waiting for transfers between devices: 170 us -> none  [the longest x1 76.9 us: per_device(): rotation_full = lax.all_gather(rotation, DP, axis=0, tiled=True)]
    pallas_call x0 -> x2, Pallas kernels: none -> 124 us  [the longest x1 63 us: rotate(): pl.pallas_call(rotate_kernel, out_shape=jax.ShapeDtypeStruct((total, dept...]
    unnamed x15 -> x2, local copies, waits for them, and re-layouts: 26.5 us -> 0.01 us
    dot_general x1 -> x0, matrix products: 15 us -> none  [per_device(): product = jnp.dot(left, rotation_full, preferred_element_type=jnp.float32)]
    slice x1, local copies, waits for them, and re-layouts: 6.87 us -> 1 us  [per_device(): turned = product[rows:].reshape(layers, 2, part, width)]
  transfers between devices with their start and end apart: 3 -> 0, of which waited for: 3 -> 0; matrix products, arithmetic and copies ran while one was open for 4% -> 0% of each run, Pallas kernels for 10% -> 0%
where the time goes in v2:
time: 272 us; the launch traced here: 271 us
  Pallas kernels  258 us (95%)
  other arithmetic  7.33 us (3%)
  between operations  3.2 us (1%)
  local copies, waits for them, and re-layouts  2.92 us (1%)
    pallas_call x1, Pallas kernels, rotate(): pl.pallas_call(rotate_kernel, out_shape=jax.ShapeDtypeStruct((total, dept...  63 us
    pallas_call x1, Pallas kernels, spread(): pl.pallas_call(spread_kernel, out_shape=jax.ShapeDtypeStruct((RING, RING,...  61.1 us
    pallas_call x4, Pallas kernels, exchange(): pl.pallas_call(functools.partial(exchange_kernel, combine), out_shape=jax...  54.5 us
    pallas_call x1, Pallas kernels, second_pass(): pl.pallas_call(second_kernel, grid=(rows // ROW_STEP,), in_specs=[SCALAR,...  38.1 us
    pallas_call x1, Pallas kernels, first_pass(): pl.pallas_call(first_kernel, grid=(rows // ROW_STEP,), in_specs=[SCALAR,...  24.6 us
    pallas_call x1, Pallas kernels, last_pass(): pl.pallas_call(last_kernel, grid=(rows // ROW_STEP,), in_specs=[SCALAR, r...  16.2 us

profile of v2, /device:TPU:0, one launch (start us, length us, event | category | flops | bytes accessed | tf_op | source)
XLA Modules:
  0.0 271.0 jit_solution(18196165043446047703)
XLA Ops:
  0.6 1.2 dynamic_slice.3.len_ref
  1.9 0.9 fusion.14
  2.8 0.9 pad_maximum_fusion
  3.7 0.7 copy.8
  4.4 63.0 %shard_map.77.resid_ref = f32[800,2560]{1,0:T(8,128)} custom-call(bf16[20,2560]{1,0:T(8,128)(2,1)} %rotation_ref.1, bf16[768,2560]{1,0:T(8,128)(2,1)} %hidden_ref.1, bf16[32,2560]{1,0:T(8,128)(2,1)} %bitcast.18), custom_call_target="tpu_custom_call" | custom-call | tf_op jit(solution)/shard_map/pallas_call | solution.py:271
  67.4 1.0 slice.12
  68.4 0.7 abs_reduce_fusion.1
  69.0 15.9 %shard_map.78 = f32[2,2560]{1,0:T(2,128)} custom-call(f32[2,2560]{1,0:T(2,128)} %get-tuple-element.25.x_ref), custom_call_target="tpu_custom_call" | custom-call | tf_op jit(solution)/shard_map/pallas_call | solution.py:74
  85.0 0.7 multiply_add_fusion
  85.8 0.2 fusion.13
  86.0 0.7 pad_maximum_fusion.1
  86.7 61.1 %shard_map.79 = bf16[4,4,4,64,2560]{4,3,2,1,0:T(8,128)(2,1)} custom-call(bf16[4,8,2560]{2,1,0:T(8,128)(2,1)} %bitcast.17), custom_call_target="tpu_custom_call" | custom-call | tf_op jit(solution)/shard_map/pallas_call | solution.py:331
  147.8 24.6 %shard_map.80 = (f32[768,1024]{1,0:T(8,128)}, f32[768,1]{1,0:T(8,128)}, f32[768,1]{1,0:T(8,128)}, f32[1,1024]{1,0:T(1,128)}) custom-call(s32[1]{0:T(128)} %dynamic_slice.3.len_ref, f32[800,2560]{1,0:T(8,128)} %shard_map.77.resid_ref, bf16[64,64,2560]{2,1,0:T(8,128)(2,1)} %bitcast.11), custom_call_target="tpu_custom_call" | custom-call | tf_op jit(solution)/shard_map/pallas_call | solution.py:487
  172.4 13.1 %shard_map.81 = f32[1,1024]{1,0:T(1,128)} custom-call(f32[1,1024]{1,0:T(1,128)} %get-tuple-element.14.x_ref), custom_call_target="tpu_custom_call" | custom-call | tf_op jit(solution)/shard_map/pallas_call | solution.py:74
  185.4 1.3 multiply_add_fusion.2
  186.7 38.1 %shard_map.82 = (f32[768,2560]{1,0:T(8,128)}, f32[768,1024]{1,0:T(8,128)}, f32[768,1]{1,0:T(8,128)}, f32[768,1]{1,0:T(8,128)}, f32[1,1024]{1,0:T(1,128)}) custom-call(s32[1]{0:T(128)} %dynamic_slice.3.len_ref, f32[800,2560]{1,0:T(8,128)} %shard_map.77.resid_ref, f32[768,1024]{1,0:T(8,128)} %get-tuple-element.13.mixed_ref, ...), custom_call_target="tpu_custom_call" | custom-call | tf_op jit(solution)/shard_map/pallas_call | solution.py:504
  224.9 13.0 %shard_map.83 = f32[1,1024]{1,0:T(1,128)} custom-call(f32[1,1024]{1,0:T(1,128)} %get-tuple-element.19.x_ref), custom_call_target="tpu_custom_call" | custom-call | tf_op jit(solution)/shard_map/pallas_call | solution.py:74
  237.8 1.3 multiply_add_fusion.1
  239.1 0.0 copy-start
  239.1 16.2 %shard_map.84 = (bf16[768,2560]{1,0:T(8,128)(2,1)}, f32[1,128]{1,0:T(1,128)}) custom-call(s32[1]{0:T(128)} %dynamic_slice.3.len_ref, f32[768,2560]{1,0:T(8,128)} %get-tuple-element.17.resid_ref, f32[768,1024]{1,0:T(8,128)} %get-tuple-element.18.mixed_ref, f32[1,1024]{1,0:T(1,128)} %get-tuple-element.29.gain_ref, f32[1,1024]{1,0:T(1,128)} %get-tuple-element.28.step_ref, ...), custom_call_target="tpu_custom_call" | custom-call | tf_op jit(solution)/shard_map/pallas_call | solution.py:525
  255.3 12.5 %shard_map.85 = f32[1,128]{1,0:T(1,128)} custom-call(f32[1,128]{1,0:T(1,128)} %get-tuple-element.23.x_ref), custom_call_target="tpu_custom_call" | custom-call | tf_op jit(solution)/shard_map/pallas_call | solution.py:74
  267.8 0.0 copy-done
  267.9 0.6 reduce_sum.9
  (1 shorter events, 0.0 us)
Async XLA Ops:
  239.1 28.7 %copy-start = (s32[128]{0:T(128)S(1)}, s32[128]{0:T(128)}, u32[]{:S(2)}) copy-start(s32[128]{0:T(128)} %param.11) | copy-start | bytes 1540

commit v3 on v2

v3 whole, which is shorter than its diff:
```python
import functools

import jax
import jax.numpy as jnp
from jax import lax
from jax.experimental import pallas as pl
from jax.experimental.pallas import tpu as pltpu
from jax.sharding import Mesh
from jax.sharding import PartitionSpec as P

DP = ("dp_0", "dp_1", "dp_2", "dp_3")
EPS_NORM = 1e-06
EPS_SCALE = 1e-06
CLIP_RATIO = 0.9
SOFT = (6.579714691285096, -12.986868668454669, 12.191614515303863, -6.570949514891455, 1.970640660123473)
ROW_STEP = 256
SUB = 64
VMEM_LIMIT = 60 * 1024 * 1024
MESH_ID = pl.DeviceIdType.MESH


def soft_round(values):
    whole = jnp.round(values)
    rest = values - whole
    square = rest * rest
    poly = SOFT[4] * square + SOFT[3]
    for coefficient in (SOFT[2], SOFT[1], SOFT[0]):
        poly = poly * square + coefficient
    return whole + (rest * square) * poly


def fake_quant(values, step_size):
    return soft_round(jnp.clip(values / step_size, -8.0, 7.0)) * step_size


RING = 4
COLORS = ((0, 1, 2), (1, 2, 0), (2, 0, 1))
PER_COLOR = 24


def places():
    return [lax.axis_index(name) for name in DP]


def neighbours(place):
    ids = []
    for axis in range(3):
        for shift in (1, RING - 1):
            ids.append({DP[axis]: lax.rem(place[axis] + shift, RING)})
    ids.append({DP[3]: 1 - place[3]})
    return ids


def greet(place):
    barrier = pltpu.get_barrier_semaphore()
    ids = neighbours(place)
    for peer in ids:
        pl.semaphore_signal(barrier, inc=1, device_id=peer, device_id_type=MESH_ID)
    return lambda: pl.semaphore_wait(barrier, len(ids))


class Gather:
    def __init__(self, buffer, place, send, recv, first_row, rows, first_column, widths):
        self.buffer, self.place, self.send, self.recv = buffer, place, send, recv
        self.half = buffer.shape[4] // 2
        self.first_row, self.rows = first_row, rows
        self.first_column, self.widths = first_column, widths
        self.partner = {DP[3]: 1 - place[3]}
        self.pending = []
        self.counter = 0

    def view(self, color, position, axis, done, part=None):
        start = self.first_column + sum(self.widths[:color])
        cols = pl.ds(pl.multiple_of(self.place[3] * self.half + start, 128), self.widths[color])
        index = [self.place[k] for k in range(3)]
        for k in done:
            index[k] = slice(None)
        index[axis] = position
        rows = pl.ds(self.first_row, self.rows)
        if part is not None:
            if done:
                index[done[0]] = pl.ds(2 * part, 2)
            else:
                cut = (self.rows // 2 + 7) // 8 * 8
                rows = pl.ds(self.first_row, cut) if part == 0 else pl.ds(self.first_row + cut, self.rows - cut)
        return self.buffer.at[index[0], index[1], index[2], rows, cols]

    def copy(self, view, peer):
        slot = self.counter
        self.counter += 1
        copy = pltpu.make_async_remote_copy(
            src_ref=view, dst_ref=view, send_sem=self.send.at[slot], recv_sem=self.recv.at[slot],
            device_id=peer, device_id_type=MESH_ID,
        )
        copy.start()
        self.pending.append((copy, peer is self.partner))
        return copy

    def steps(self):
        state = {}

        def begin(phase):
            for color, order in enumerate(COLORS):
                axis, done = order[phase], order[:phase]
                own = self.place[axis]
                up = {DP[axis]: lax.rem(own + 1, RING)}
                down = {DP[axis]: lax.rem(own + RING - 1, RING)}
                block = self.view(color, own, axis, done)
                state[phase, color] = [self.copy(block, up), self.copy(block, down)]

        def relay(phase):
            for color, order in enumerate(COLORS):
                axis, done = order[phase], order[:phase]
                own = self.place[axis]
                above, below = lax.rem(own + 1, RING), lax.rem(own + RING - 1, RING)
                from_below, from_above = state[phase, color]
                from_below.wait_recv()
                first = self.copy(self.view(color, below, axis, done, 0), {DP[axis]: above})
                self.copy(self.view(color, below, axis, done), self.partner)
                from_above.wait_recv()
                second = self.copy(self.view(color, above, axis, done, 1), {DP[axis]: below})
                self.copy(self.view(color, above, axis, done), self.partner)
                state[phase, color] = [first, second]

        def finish(phase):
            for color, order in enumerate(COLORS):
                axis, done = order[phase], order[:phase]
                across = lax.rem(self.place[axis] + 2, RING)
                for copy in state[phase, color]:
                    copy.wait_recv()
                self.copy(self.view(color, across, axis, done), self.partner)

        result = []
        for phase in range(3):
            if phase == 0:
                result.append(lambda: begin(0))
            result.append(functools.partial(relay, phase))
            if phase < 2:
                def turn(phase=phase):
                    finish(phase)
                    begin(phase + 1)
                result.append(turn)
            else:
                result.append(functools.partial(finish, phase))
        result.append(self.drain)
        return result

    def drain(self):
        for copy, kept in self.pending:
            copy.wait_send()
            if kept:
                copy.wait_recv()


def rotate_kernel(rotation_ref, hidden_ref, weight_ref, product_ref, full, left, pair, wide, send, recv, pair_send, pair_recv, local):
    place = places()
    ready = greet(place)
    rows = rotation_ref.shape[0]
    tokens = hidden_ref.shape[0]
    loads = [
        pltpu.make_async_copy(hidden_ref, left.at[pl.ds(0, tokens)], local.at[0]),
        pltpu.make_async_copy(weight_ref, left.at[pl.ds(tokens, weight_ref.shape[0])], local.at[1]),
    ]
    for load in loads:
        load.start()
    core = place[3]
    ready()
    swap = pltpu.make_async_remote_copy(
        src_ref=rotation_ref, dst_ref=pair.at[core], send_sem=pair_send, recv_sem=pair_recv,
        device_id={DP[3]: 1 - core}, device_id_type=MESH_ID,
    )
    swap.start()
    pair[core] = rotation_ref[...]
    swap.wait()
    for k in range(2):
        wide[k * rows : (k + 1) * rows, :] = pair[k].astype(jnp.float32)
    full[place[0], place[1], place[2]] = wide[...].astype(jnp.bfloat16)
    early = Gather(full, place, send.at[0], recv.at[0], 0, 2 * rows, 0, (256, 256, 256))
    late = Gather(full, place, send.at[1], recv.at[1], 0, 2 * rows, 768, (256, 128, 128))
    one, two = early.steps(), late.steps()
    for k in range(4):
        one[k]()
        two[k]()
    one[4]()
    one[5]()
    two[4]()
    for load in loads:
        load.wait()
    depth = left.shape[1]
    width = 256

    def columns(first, count):
        def body(index, carry):
            for core_half in range(2):
                cols = pl.ds(pl.multiple_of(core_half * (depth // 2) + first + index * width, width), width)
                block = full[:, :, :, :, cols].reshape(depth, width)
                product_ref[:, cols] = jnp.dot(left[...], block, preferred_element_type=jnp.float32)
            return carry

        lax.fori_loop(0, count, body, 0)

    one[6]()
    one[7]()
    columns(0, 2)
    two[5]()
    columns(512, 1)
    two[6]()
    two[7]()
    columns(768, 2)


def rotate(rotation, hidden, weights):
    rows, depth = rotation.shape
    total = hidden.shape[0] + weights.shape[0]
    return pl.pallas_call(
        rotate_kernel,
        out_shape=jax.ShapeDtypeStruct((total, depth), jnp.float32),
        in_specs=[
            pl.BlockSpec(memory_space=pltpu.VMEM),
            pl.BlockSpec(memory_space=pl.ANY),
            pl.BlockSpec(memory_space=pl.ANY),
        ],
        out_specs=pl.BlockSpec(memory_space=pltpu.VMEM),
        scratch_shapes=[
            pltpu.VMEM((RING, RING, RING, 2 * rows, depth), jnp.bfloat16),
            pltpu.VMEM((total, depth), jnp.bfloat16),
            pltpu.VMEM((2, rows, depth), jnp.bfloat16),
            pltpu.VMEM((2 * rows, depth), jnp.float32),
            pltpu.SemaphoreType.DMA((2, 63)),
            pltpu.SemaphoreType.DMA((2, 63)),
            pltpu.SemaphoreType.DMA,
            pltpu.SemaphoreType.DMA,
            pltpu.SemaphoreType.DMA((2,)),
        ],
        compiler_params=pltpu.CompilerParams(
            collective_id=3, has_side_effects=True, vmem_limit_bytes=VMEM_LIMIT
        ),
    )(rotation, hidden, weights)


NEAR = [(dy, dc) for dy in range(4) for dc in range(2) if (dy, dc) != (0, 0)]
FAR = [(dx, dz) for dx in range(4) for dz in range(4) if (dx, dz) != (0, 0)]


def near_peers(place):
    return [{DP[2]: lax.rem(place[2] + dy, 4), DP[3]: lax.rem(place[3] + dc, 2)} for dy, dc in NEAR]


def far_peers(place):
    return [{DP[0]: lax.rem(place[0] + dx, 4), DP[1]: lax.rem(place[1] + dz, 4)} for dx, dz in FAR]


class Exchange:
    def __init__(self, combine, place, buffers):
        self.combine, self.place = combine, place
        self.source, self.near, self.mid, self.far = buffers[:4]
        self.near_send, self.near_recv, self.far_send, self.far_recv = buffers[4:]

    def share(self, source, slots, me, peers, send, recv):
        slots[me] = source[...]
        copies = [
            pltpu.make_async_remote_copy(
                src_ref=source, dst_ref=slots.at[me], send_sem=send.at[k], recv_sem=recv.at[k],
                device_id=peer, device_id_type=MESH_ID,
            )
            for k, peer in enumerate(peers)
        ]
        for copy in copies:
            copy.start()
        return copies

    def total(self, slots, copies):
        for copy in copies:
            copy.wait()
        result = slots[0]
        for k in range(1, slots.shape[0]):
            result = self.combine(result, slots[k])
        return result

    def start(self, value):
        self.source[...] = value
        me = self.place[2] * 2 + self.place[3]
        self.copies = self.share(self.source, self.near, me, near_peers(self.place), self.near_send, self.near_recv)

    def turn(self):
        self.mid[...] = self.total(self.near, self.copies)
        me = self.place[0] * 4 + self.place[1]
        self.copies = self.share(self.mid, self.far, me, far_peers(self.place), self.far_send, self.far_recv)

    def finish(self):
        return self.total(self.far, self.copies)


def exchange_scratch(shape):
    return [
        pltpu.VMEM(shape, jnp.float32),
        pltpu.VMEM((8,) + shape, jnp.float32),
        pltpu.VMEM(shape, jnp.float32),
        pltpu.VMEM((16,) + shape, jnp.float32),
        pltpu.SemaphoreType.DMA((len(NEAR),)),
        pltpu.SemaphoreType.DMA((len(NEAR),)),
        pltpu.SemaphoreType.DMA((len(FAR),)),
        pltpu.SemaphoreType.DMA((len(FAR),)),
    ]


def quantize_rows(resid, act, square, error, first, count):
    width = resid.shape[1]

    def step(index, carry):
        rows = pl.ds(pl.multiple_of(first + index * SUB, SUB), SUB)
        squares = jnp.zeros((SUB, 128), jnp.float32)
        tops = jnp.zeros((SUB, 128), jnp.float32)
        for start in range(0, width, 128):
            part = resid[rows, start : start + 128]
            squares = squares + part * part
            tops = jnp.maximum(tops, jnp.abs(part))
        mean_sq = jnp.sum(squares, axis=1, keepdims=True) / width
        scale = lax.rsqrt(mean_sq + EPS_NORM)
        step_size = CLIP_RATIO * (jnp.max(tops, axis=1, keepdims=True) * scale) / 7.0 + EPS_SCALE
        gain = jnp.broadcast_to(scale / step_size, (SUB, 128))
        wide_step = jnp.broadcast_to(step_size, (SUB, 128))
        errors = jnp.zeros((SUB, 128), jnp.float32)
        for start in range(0, width, 128):
            units = resid[rows, start : start + 128] * gain
            rounded = soft_round(jnp.minimum(jnp.maximum(units, -8.0), 7.0))
            gap = rounded - units
            errors = errors + gap * gap
            act[rows, start : start + 128] = (rounded * wide_step).astype(jnp.bfloat16)
        square[rows, :] = mean_sq
        error[rows, :] = jnp.sum(errors, axis=1, keepdims=True) * (step_size * step_size)
        return carry

    lax.fori_loop(0, count // SUB, step, 0)


def quantize_mixed(mixed, gain, step_size, mix, error, first, count):
    channels = mixed.shape[1]

    def step(index, carry):
        rows = pl.ds(pl.multiple_of(first + index * SUB, SUB), SUB)
        errors = jnp.zeros((SUB, 128), jnp.float32)
        for start in range(0, channels, 128):
            cols = slice(start, start + 128)
            units = mixed[rows, cols] * gain[:, cols]
            rounded = soft_round(jnp.minimum(jnp.maximum(units, -8.0), 7.0))
            gap = (rounded - units) * step_size[:, cols]
            errors = errors + gap * gap
            mix[rows, cols] = (rounded * step_size[:, cols]).astype(jnp.bfloat16)
        error[rows, :] = jnp.sum(errors, axis=1, keepdims=True)
        return carry

    lax.fori_loop(0, count // SUB, step, 0)


def layers_kernel(
    len_ref, product_ref, out_ref, sum_ref,
    full, resid, act, mixed, mix, pair, turned, square, error, loss, top, gain, step_size,
    ring_send, ring_recv, swap_send, swap_recv, local, *exchanges,
):
    place = places()
    core = place[3]
    tokens, width = resid.shape
    channels = mixed.shape[1]
    part = pair.shape[2]
    barrier = pltpu.get_barrier_semaphore()
    peers = near_peers(place) + far_peers(place)
    for peer in peers:
        pl.semaphore_signal(barrier, inc=1, device_id=peer, device_id_type=MESH_ID)
    loads = [
        pltpu.make_async_copy(product_ref.at[pl.ds(tokens, 4 * part)], turned, local.at[0]),
        pltpu.make_async_copy(product_ref.at[pl.ds(0, tokens)], resid, local.at[1]),
    ]
    for load in loads:
        load.start()
    tops_max = Exchange(jnp.maximum, place, exchanges[0:8])
    ranges = [Exchange(jnp.maximum, place, exchanges[8:16]), Exchange(jnp.maximum, place, exchanges[16:24])]
    loss_sum = Exchange(jnp.add, place, exchanges[24:32])

    def matrix(which):
        return turned[which * part : (which + 1) * part, :]

    def swap(first):
        copy = pltpu.make_async_remote_copy(
            src_ref=pair.at[core, pl.ds(first, 2)], dst_ref=pair.at[core, pl.ds(first, 2)],
            send_sem=swap_send.at[first // 2], recv_sem=swap_recv.at[first // 2],
            device_id={DP[3]: 1 - core}, device_id_type=MESH_ID,
        )
        copy.start()
        return copy

    def combine(first):
        for k in (first, first + 1):
            both = jnp.concatenate([pair[0, k].astype(jnp.float32), pair[1, k].astype(jnp.float32)], axis=0)
            full[place[0], place[1], place[2], 2 * part * k : 2 * part * (k + 1), :] = both.astype(jnp.bfloat16)

    def weights(which):
        return full[:, :, :, 2 * part * which : 2 * part * (which + 1), :].reshape(channels, width)

    loads[0].wait()
    for k in range(2):
        value = matrix(k)
        value_top = jnp.max(jnp.abs(value), axis=1, keepdims=True)
        pair[core, k] = fake_quant(value, value_top / 7.0 + EPS_SCALE).astype(jnp.bfloat16)
    output_tops = jnp.concatenate(
        [jnp.max(jnp.abs(matrix(k)), axis=0, keepdims=True) for k in (2, 3)], axis=0
    )
    pl.semaphore_wait(barrier, len(peers))
    swapped = swap(0)
    tops_max.start(output_tops)
    values = Gather(full, place, ring_send.at[0], ring_recv.at[0], 0, 4 * part, 0, (512, 384, 384)).steps()
    outputs = Gather(full, place, ring_send.at[1], ring_recv.at[1], 4 * part, 4 * part, 0, (384, 512, 384)).steps()
    loads[1].wait()
    swapped.wait()
    combine(0)
    done = 0

    def rows_ahead(count):
        nonlocal done
        quantize_rows(resid, act, square, error, done, count)
        done = done + count

    values[0]()
    rows_ahead(128)
    values[1]()
    tops_max.turn()
    rows_ahead(64)
    values[2]()
    rows_ahead(128)
    values[3]()
    tops = tops_max.finish()
    for k in (2, 3):
        step = tops[k - 2 : k - 1, :] / 7.0 + EPS_SCALE
        pair[core, k] = fake_quant(matrix(k), step).astype(jnp.bfloat16)
    swapped = swap(2)
    rows_ahead(64)
    swapped.wait()
    combine(2)
    values[4]()
    outputs[0]()
    rows_ahead(128)
    outputs[1]()
    rows_ahead(128)
    outputs[2]()
    rows_ahead(128)
    outputs[3]()
    values[5]()
    outputs[4]()
    values[6]()
    values[7]()

    def live_rows(first, count):
        return first + lax.broadcasted_iota(jnp.int32, (count, 1), 0) < len_ref[0]

    def mix_block(first, which):
        rows = pl.ds(pl.multiple_of(first, ROW_STEP), ROW_STEP)
        block = lax.dot_general(
            act[rows, :], weights(which), (((1,), (1,)), ((), ())), preferred_element_type=jnp.float32
        )
        mixed[rows, :] = block
        seen = jnp.where(live_rows(first, ROW_STEP), jnp.abs(block), 0.0)
        top[...] = jnp.maximum(top[...], jnp.max(seen.reshape(ROW_STEP // 8, 8, channels), axis=0))

    def set_steps(vrange):
        sizes = CLIP_RATIO * vrange / 7.0 + EPS_SCALE
        step_size[...] = sizes
        gain[...] = 1.0 / sizes

    top[...] = jnp.zeros_like(top)
    loss[...] = square[...] * error[...]
    blocks = tokens // ROW_STEP
    lax.fori_loop(0, 1, lambda i, c: (mix_block(i * ROW_STEP, 0), c)[1], 0)
    outputs[5]()
    lax.fori_loop(1, blocks, lambda i, c: (mix_block(i * ROW_STEP, 0), c)[1], 0)
    ranges[0].start(jnp.max(top[...], axis=0, keepdims=True))
    outputs[6]()
    ranges[0].turn()
    outputs[7]()
    set_steps(ranges[0].finish())
    top[...] = jnp.zeros_like(top)

    def middle(index, carry):
        first = index * ROW_STEP
        rows = pl.ds(pl.multiple_of(first, ROW_STEP), ROW_STEP)
        quantize_mixed(mixed, gain, step_size, mix, error, first, ROW_STEP)
        loss[rows, :] = loss[rows, :] + square[rows, :] * error[rows, :]
        resid[rows, :] = resid[rows, :] + jnp.dot(mix[rows, :], weights(2), preferred_element_type=jnp.float32)
        quantize_rows(resid, act, square, error, first, ROW_STEP)
        loss[rows, :] = loss[rows, :] + square[rows, :] * error[rows, :]
        mix_block(first, 1)
        return carry

    lax.fori_loop(0, blocks, middle, 0)
    ranges[1].start(jnp.max(top[...], axis=0, keepdims=True))
    ranges[1].turn()
    set_steps(ranges[1].finish())
    quantize_mixed(mixed, gain, step_size, mix, error, 0, tokens)
    kept = jnp.where(live_rows(0, tokens), loss[...] + square[...] * error[...], 0.0)
    loss_sum.start(jnp.broadcast_to(jnp.sum(kept, axis=0, keepdims=True), sum_ref.shape))

    def last(index, carry):
        first = index * ROW_STEP
        rows = pl.ds(pl.multiple_of(first, ROW_STEP), ROW_STEP)
        updated = resid[rows, :] + jnp.dot(mix[rows, :], weights(3), preferred_element_type=jnp.float32)
        out_ref[rows, :] = jnp.where(live_rows(first, ROW_STEP), updated, 0.0).astype(jnp.bfloat16)
        return carry

    lax.fori_loop(0, 1, last, 0)
    loss_sum.turn()
    lax.fori_loop(1, blocks, last, 0)
    sum_ref[...] = loss_sum.finish()


def run_layers(own_len, product, tokens, channels, part):
    width = product.shape[1]
    column = pltpu.VMEM((tokens, 1), jnp.float32)
    scratch = [
        pltpu.VMEM((RING, RING, RING, 8 * part, width), jnp.bfloat16),
        pltpu.VMEM((tokens, width), jnp.float32),
        pltpu.VMEM((tokens, width), jnp.bfloat16),
        pltpu.VMEM((tokens, channels), jnp.float32),
        pltpu.VMEM((tokens, channels), jnp.bfloat16),
        pltpu.VMEM((2, 4, part, width), jnp.bfloat16),
        pltpu.VMEM((4 * part, width), jnp.float32),
        column, column, column,
        pltpu.VMEM((8, channels), jnp.float32),
        pltpu.VMEM((1, channels), jnp.float32),
        pltpu.VMEM((1, channels), jnp.float32),
        pltpu.SemaphoreType.DMA((2, 63)),
        pltpu.SemaphoreType.DMA((2, 63)),
        pltpu.SemaphoreType.DMA((2,)),
        pltpu.SemaphoreType.DMA((2,)),
        pltpu.SemaphoreType.DMA((2,)),
    ]
    for shape in ((2, width), (1, channels), (1, channels), (1, 128)):
        scratch = scratch + exchange_scratch(shape)
    vmem = pl.BlockSpec(memory_space=pltpu.VMEM)
    return pl.pallas_call(
        layers_kernel,
        out_shape=[
            jax.ShapeDtypeStruct((tokens, width), jnp.bfloat16),
            jax.ShapeDtypeStruct((1, 128), jnp.float32),
        ],
        in_specs=[pl.BlockSpec(memory_space=pltpu.SMEM), pl.BlockSpec(memory_space=pl.ANY)],
        out_specs=[vmem, vmem],
        scratch_shapes=scratch,
        compiler_params=pltpu.CompilerParams(collective_id=4, has_side_effects=True, vmem_limit_bytes=VMEM_LIMIT),
    )(own_len, product)


def per_device(hidden, rotation, norm_gain, value_weight, output_weight, lengths):
    tokens, width = hidden.shape
    layers, part = output_weight.shape[0], output_weight.shape[1]
    scaled = (norm_gain[:, :, None] * value_weight.astype(jnp.float32)).astype(jnp.bfloat16)
    own = jnp.concatenate([jnp.transpose(scaled, (0, 2, 1)), output_weight], axis=0)
    product = rotate(rotation, hidden, own.reshape(2 * layers * part, width))
    own_len = lax.dynamic_slice_in_dim(lengths, lax.axis_index(DP), 1)
    out, total = run_layers(own_len, product, tokens, part * lax.axis_size(DP), part)
    count = jnp.sum(lengths).astype(jnp.float32)
    return out, total[0, 0] / count


def solution(mesh):
    finer = Mesh(mesh.devices.reshape(4, 4, 4, 2), DP)
    in_specs = (P(DP, None), P(DP, None), P(), P(None, None, DP), P(None, DP, None), P())
    out_specs = (P(DP, None), P())
    return jax.shard_map(per_device, mesh=finer, in_specs=in_specs, out_specs=out_specs, check_vma=False)
```

time: 272 us -> 192 us (0.71)
  Pallas kernels: 258 us -> 180 us
  other arithmetic: 7.33 us -> 3.11 us
    pallas_call x8 -> x1, Pallas kernels: 195 us -> 117 us  [run_layers(): pl.pallas_call(layers_kernel, out_shape=[jax.ShapeDtypeStruct((tokens, wi...]
    unnamed x2 -> x3, local copies, waits for them, and re-layouts: 0.01 us -> 4.3 us
    add x4 -> x0, other arithmetic: 3.3 us -> none  [the longest x2 2.56 us: mix_scale(): step_size = CLIP_RATIO * exchange(jnp.maximum, top, 1) / 7.0 + EPS_SCALE]
where the time goes in v3:
time: 192 us
  Pallas kernels  180 us (94%)
  local copies, waits for them, and re-layouts  5.54 us (3%)
  other arithmetic  3.11 us (2%)
  between operations  3.02 us (2%)
    pallas_call x1, Pallas kernels, run_layers(): pl.pallas_call(layers_kernel, out_shape=[jax.ShapeDtypeStruct((tokens, wi...  117 us
    pallas_call x1, Pallas kernels, rotate(): pl.pallas_call(rotate_kernel, out_shape=jax.ShapeDtypeStruct((total, dept...  62.9 us
    unnamed x3, local copies, waits for them, and re-layouts  4.3 us

profile of v3, /device:TPU:0, one launch (start us, length us, event | category | flops | bytes accessed | tf_op | source)
XLA Modules:
  0.0 191.5 jit_solution(1247218662792599002)
XLA Ops:
  0.6 1.2 dynamic_slice.3.len_ref
  1.9 0.9 fusion
  2.8 1.6 maximum_bitcast_fusion.weight_ref
  4.4 62.9 %shard_map.77.product_ref = f32[800,2560]{1,0:T(8,128)} custom-call(bf16[20,2560]{1,0:T(8,128)(2,1)} %rotation_ref.1, bf16[768,2560]{1,0:T(8,128)(2,1)} %hidden_ref.1, bf16[32,2560]{1,0:T(8,128)(2,1)} %maximum_bitcast_fusion.weight_ref), custom_call_target="tpu_custom_call" | custom-call | tf_op jit(solution)/shard_map/pallas_call | solution.py:215
  67.3 0.0 copy-start
  67.3 116.9 %shard_map.78 = (bf16[768,2560]{1,0:T(8,128)(2,1)}, f32[1,128]{1,0:T(1,128)}) custom-call(s32[1]{0:T(128)} %dynamic_slice.3.len_ref, f32[800,2560]{1,0:T(8,128)} %shard_map.77.product_ref), custom_call_target="tpu_custom_call" | custom-call | tf_op jit(solution)/shard_map/pallas_call | solution.py:538
  184.2 0.0 copy-done
  184.3 0.6 reduce_sum.9
  186.1 4.3 %copy.9 = bf16[768,2560]{1,0:T(8,128)(2,1)} copy(bf16[768,2560]{1,0:T(8,128)(2,1)} %get-tuple-element.8) | data formatting | bytes 7864320
Async XLA Ops:
  67.3 117.0 %copy-start = (s32[128]{0:T(128)S(1)}, s32[128]{0:T(128)}, u32[]{:S(2)}) copy-start(s32[128]{0:T(128)} %param.11) | copy-start | bytes 1540

commit v4 on v3

v4 whole, which is shorter than its diff:
```python
import functools

import jax
import jax.numpy as jnp
from jax import lax
from jax.experimental import pallas as pl
from jax.experimental.pallas import tpu as pltpu
from jax.sharding import Mesh
from jax.sharding import PartitionSpec as P

DP = ("dp_0", "dp_1", "dp_2", "dp_3")
EPS_NORM = 1e-06
EPS_SCALE = 1e-06
CLIP_RATIO = 0.9
SOFT = (6.579714691285096, -12.986868668454669, 12.191614515303863, -6.570949514891455, 1.970640660123473)
ROW_STEP = 256
SUB = 64
VMEM_LIMIT = 63 * 1024 * 1024
MESH_ID = pl.DeviceIdType.MESH


def soft_round(values):
    whole = jnp.round(values)
    rest = values - whole
    square = rest * rest
    poly = SOFT[4] * square + SOFT[3]
    for coefficient in (SOFT[2], SOFT[1], SOFT[0]):
        poly = poly * square + coefficient
    return whole + (rest * square) * poly


def fake_quant(values, step_size):
    return soft_round(jnp.clip(values / step_size, -8.0, 7.0)) * step_size


RING = 4
COLORS = ((0, 1, 2), (1, 2, 0), (2, 0, 1))


class Gather:
    def __init__(self, buffer, place, send, recv, first_row, rows, parts, first_column, widths):
        self.buffer, self.place, self.send, self.recv = buffer, place, send, recv
        self.half = buffer.shape[4] // 2
        self.first_row, self.rows, self.parts = first_row, rows, parts
        self.first_column, self.widths = first_column, widths
        self.partner = {DP[3]: 1 - place[3]}
        self.pending = {None: []}
        self.state = {}
        self.counter = 0

    def view(self, color, position, phase, part, side=None):
        order = COLORS[color]
        done = order[:phase]
        start = self.first_column + sum(self.widths[:color])
        cols = pl.ds(pl.multiple_of(self.place[3] * self.half + start, 128), self.widths[color])
        index = [self.place[k] for k in range(3)]
        for k in done:
            index[k] = slice(None)
        index[order[phase]] = position
        if side is not None:
            index[done[0]] = pl.ds(2 * side, 2)
        rows = pl.ds(self.first_row, self.rows)
        if part is not None:
            count = self.rows // self.parts
            rows = pl.ds(self.first_row + part * count, count)
        return self.buffer.at[index[0], index[1], index[2], rows, cols]

    def copy(self, view, peer, part):
        slot = self.counter
        self.counter += 1
        copy = pltpu.make_async_remote_copy(
            src_ref=view, dst_ref=view, send_sem=self.send.at[slot], recv_sem=self.recv.at[slot],
            device_id=peer, device_id_type=MESH_ID,
        )
        copy.start()
        self.pending.setdefault(part, []).append((copy, peer is self.partner))
        return copy

    def ring(self, color, phase):
        axis = COLORS[color][phase]
        own = self.place[axis]
        return axis, own, lax.rem(own + 1, RING), lax.rem(own + 2, RING), lax.rem(own + RING - 1, RING)

    def begin(self, phase, part=None):
        for color in range(3):
            axis, own, above, across, below = self.ring(color, phase)
            block = self.view(color, own, phase, part)
            copies = [self.copy(block, {DP[axis]: above}, part), self.copy(block, {DP[axis]: below}, part)]
            if phase == 0:
                copies.append(self.copy(block, {DP[axis]: across}, part))
            self.state[phase, color, part] = copies

    def relay(self, phase, part=None):
        for color in range(3):
            axis, own, above, across, below = self.ring(color, phase)
            from_below, from_above = self.state[phase, color, part]
            from_below.wait_recv()
            first = self.copy(self.view(color, below, phase, part, 0), {DP[axis]: above}, part)
            self.copy(self.view(color, below, phase, part), self.partner, part)
            from_above.wait_recv()
            second = self.copy(self.view(color, above, phase, part, 1), {DP[axis]: below}, part)
            self.copy(self.view(color, above, phase, part), self.partner, part)
            self.state[phase, color, part] = [first, second]

    def finish(self, phase, part=None):
        for color in range(3):
            axis, own, above, across, below = self.ring(color, phase)
            for copy in self.state[phase, color, part]:
                copy.wait_recv()
            self.copy(self.view(color, across, phase, part), self.partner, part)
            if phase == 0:
                self.copy(self.view(color, below, phase, part), self.partner, part)
                self.copy(self.view(color, above, phase, part), self.partner, part)

    def drain(self, part=None):
        for copy, kept in self.pending.pop(part, []):
            copy.wait_send()
            if kept:
                copy.wait_recv()


def gather_slots(parts):
    return 3 * (6 + 7 + 7 * parts)


NEAR = [(dy, dc) for dy in range(4) for dc in range(2) if (dy, dc) != (0, 0)]
FAR = [(dx, dz) for dx in range(4) for dz in range(4) if (dx, dz) != (0, 0)]


def near_peers(place):
    return [{DP[2]: lax.rem(place[2] + dy, 4), DP[3]: lax.rem(place[3] + dc, 2)} for dy, dc in NEAR]


def far_peers(place):
    return [{DP[0]: lax.rem(place[0] + dx, 4), DP[1]: lax.rem(place[1] + dz, 4)} for dx, dz in FAR]


class Exchange:
    def __init__(self, combine, place, buffers):
        self.combine, self.place = combine, place
        self.source, self.near, self.mid, self.far = buffers[:4]
        self.near_send, self.near_recv, self.far_send, self.far_recv = buffers[4:]

    def share(self, source, slots, me, peers, send, recv):
        slots[me] = source[...]
        copies = [
            pltpu.make_async_remote_copy(
                src_ref=source, dst_ref=slots.at[me], send_sem=send.at[k], recv_sem=recv.at[k],
                device_id=peer, device_id_type=MESH_ID,
            )
            for k, peer in enumerate(peers)
        ]
        for copy in copies:
            copy.start()
        return copies

    def total(self, slots, copies):
        for copy in copies:
            copy.wait()
        result = slots[0]
        for k in range(1, slots.shape[0]):
            result = self.combine(result, slots[k])
        return result

    def start(self, value):
        self.source[...] = value
        me = self.place[2] * 2 + self.place[3]
        self.copies = self.share(self.source, self.near, me, near_peers(self.place), self.near_send, self.near_recv)

    def turn(self):
        self.mid[...] = self.total(self.near, self.copies)
        me = self.place[0] * 4 + self.place[1]
        self.copies = self.share(self.mid, self.far, me, far_peers(self.place), self.far_send, self.far_recv)

    def finish(self):
        return self.total(self.far, self.copies)


def exchange_scratch(shape):
    return [
        pltpu.VMEM(shape, jnp.float32),
        pltpu.VMEM((8,) + shape, jnp.float32),
        pltpu.VMEM(shape, jnp.float32),
        pltpu.VMEM((16,) + shape, jnp.float32),
        pltpu.SemaphoreType.DMA((len(NEAR),)),
        pltpu.SemaphoreType.DMA((len(NEAR),)),
        pltpu.SemaphoreType.DMA((len(FAR),)),
        pltpu.SemaphoreType.DMA((len(FAR),)),
    ]


def quantize_rows(resid, act, square, error, first, count):
    width = resid.shape[1]

    def step(index, carry):
        rows = pl.ds(pl.multiple_of(first + index * SUB, SUB), SUB)
        squares = jnp.zeros((SUB, 128), jnp.float32)
        tops = jnp.zeros((SUB, 128), jnp.float32)
        for start in range(0, width, 128):
            part = resid[rows, start : start + 128]
            squares = squares + part * part
            tops = jnp.maximum(tops, jnp.abs(part))
        mean_sq = jnp.sum(squares, axis=1, keepdims=True) / width
        scale = lax.rsqrt(mean_sq + EPS_NORM)
        step_size = CLIP_RATIO * (jnp.max(tops, axis=1, keepdims=True) * scale) / 7.0 + EPS_SCALE
        gain = jnp.broadcast_to(scale / step_size, (SUB, 128))
        wide_step = jnp.broadcast_to(step_size, (SUB, 128))
        errors = jnp.zeros((SUB, 128), jnp.float32)
        for start in range(0, width, 128):
            units = resid[rows, start : start + 128] * gain
            rounded = soft_round(jnp.minimum(jnp.maximum(units, -8.0), 7.0))
            gap = rounded - units
            errors = errors + gap * gap
            act[rows, start : start + 128] = (rounded * wide_step).astype(jnp.bfloat16)
        square[rows, :] = mean_sq
        error[rows, :] = jnp.sum(errors, axis=1, keepdims=True) * (step_size * step_size)
        return carry

    lax.fori_loop(0, count // SUB, step, 0)


def quantize_mixed(mixed, gain, step_size, mix, error, first, count):
    channels = mixed.shape[1]

    def step(index, carry):
        rows = pl.ds(pl.multiple_of(first + index * SUB, SUB), SUB)
        errors = jnp.zeros((SUB, 128), jnp.float32)
        for start in range(0, channels, 128):
            cols = slice(start, start + 128)
            units = mixed[rows, cols] * gain[:, cols]
            rounded = soft_round(jnp.minimum(jnp.maximum(units, -8.0), 7.0))
            gap = (rounded - units) * step_size[:, cols]
            errors = errors + gap * gap
            mix[rows, cols] = (rounded * step_size[:, cols]).astype(jnp.bfloat16)
        error[rows, :] = jnp.sum(errors, axis=1, keepdims=True)
        return carry

    lax.fori_loop(0, count // SUB, step, 0)


def window_kernel(
    len_ref, all_len_ref, rotation_ref, value_ref, norm_ref, weight_ref, hidden_ref, out_ref, sum_ref,
    turn, full, product, left, mixed, mix, pair, wide, square, error, loss, top, gain, step_size,
    turn_send, turn_recv, ring_send, ring_recv, swap_send, swap_recv, local, *exchanges,
):
    place = [lax.axis_index(name) for name in DP]
    core = place[3]
    own_len = len_ref[((place[0] * RING + place[1]) * RING + place[2]) * 2 + core]
    tokens, width = hidden_ref.shape
    channels = mixed.shape[1]
    part = weight_ref.shape[1]
    shard = rotation_ref.shape[0]
    act = left
    barrier = pltpu.get_barrier_semaphore()
    peers = near_peers(place) + far_peers(place)
    for peer in peers:
        pl.semaphore_signal(barrier, inc=1, device_id=peer, device_id_type=MESH_ID)
    load = pltpu.make_async_copy(hidden_ref, left.at[pl.ds(0, tokens)], local.at[0])
    load.start()
    tops_max = Exchange(jnp.maximum, place, exchanges[0:8])
    ranges = [Exchange(jnp.maximum, place, exchanges[8:16]), Exchange(jnp.maximum, place, exchanges[16:24])]
    loss_sum = Exchange(jnp.add, place, exchanges[24:32])

    def swap(source, target, slot):
        copy = pltpu.make_async_remote_copy(
            src_ref=source, dst_ref=target, send_sem=swap_send.at[slot], recv_sem=swap_recv.at[slot],
            device_id={DP[3]: 1 - core}, device_id_type=MESH_ID,
        )
        copy.start()
        return copy

    both_shards = wide
    both_shards[core] = rotation_ref[...]
    small = [
        (norm_ref[k : k + 1, :] * value_ref[k].astype(jnp.float32)).astype(jnp.bfloat16).astype(jnp.float32)
        for k in range(2)
    ] + [weight_ref[k].astype(jnp.float32) for k in range(2)]
    left[tokens : tokens + 4 * part, :] = jnp.concatenate(small, axis=0).astype(jnp.bfloat16)
    pl.semaphore_wait(barrier, len(peers))
    swapped = swap(rotation_ref, both_shards.at[core], 0)
    swapped.wait()
    turn[place[0], place[1], place[2]] = jnp.concatenate(
        [both_shards[0].astype(jnp.float32), both_shards[1].astype(jnp.float32)], axis=0
    ).astype(jnp.bfloat16)
    early = Gather(turn, place, turn_send.at[0], turn_recv.at[0], 0, 2 * shard, 1, 0, (256, 256, 256))
    late = Gather(turn, place, turn_send.at[1], turn_recv.at[1], 0, 2 * shard, 1, 768, (256, 128, 128))
    chunk = 256

    def columns(first_row, rows, first, count):
        def body(index, carry):
            for core_half in range(2):
                cols = pl.ds(pl.multiple_of(core_half * (width // 2) + first + index * chunk, chunk), chunk)
                block = turn[:, :, :, :, cols].reshape(width, chunk)
                product[first_row : first_row + rows, cols] = jnp.dot(
                    left[first_row : first_row + rows, :], block, preferred_element_type=jnp.float32
                )
            return carry

        lax.fori_loop(0, count, body, 0)

    early.begin(0)
    late.begin(0)
    early.finish(0)
    early.begin(1)
    late.finish(0)
    late.begin(1)
    early.relay(1)
    late.relay(1)
    early.finish(1)
    early.begin(2)
    load.wait()
    early.relay(2)
    late.finish(1)
    late.begin(2)
    early.finish(2)
    early.drain()
    late.relay(2)
    columns(0, tokens + 4 * part, 0, 3)
    late.finish(2)
    late.drain()
    columns(tokens, 4 * part, 768, 2)

    def matrix(which):
        return product[tokens + which * part : tokens + (which + 1) * part, :]

    def combine(first):
        for k in (first, first + 1):
            both = jnp.concatenate([pair[0, k].astype(jnp.float32), pair[1, k].astype(jnp.float32)], axis=0)
            full[place[0], place[1], place[2], 2 * part * k : 2 * part * (k + 1), :] = both.astype(jnp.bfloat16)

    def weights(which):
        return full[:, :, :, 2 * part * which : 2 * part * (which + 1), :].reshape(channels, width)

    done = 0

    def rows_ahead(count):
        nonlocal done
        quantize_rows(product, act, square, error, done, count)
        done = done + count

    for k in range(2):
        value = matrix(k)
        value_top = jnp.max(jnp.abs(value), axis=1, keepdims=True)
        pair[core, k] = fake_quant(value, value_top / 7.0 + EPS_SCALE).astype(jnp.bfloat16)
    output_tops = jnp.concatenate(
        [jnp.max(jnp.abs(matrix(k)), axis=0, keepdims=True) for k in (2, 3)], axis=0
    )
    spot = pair.at[core, pl.ds(0, 2)]
    swapped = swap(spot, spot, 1)
    tops_max.start(output_tops)
    values = Gather(full, place, ring_send.at[0], ring_recv.at[0], 0, 4 * part, 2, 0, (512, 384, 384))
    outputs = Gather(full, place, ring_send.at[1], ring_recv.at[1], 4 * part, 4 * part, 2, 0, (384, 512, 384))
    swapped.wait()
    combine(0)
    values.begin(0)
    columns(0, tokens, 768, 1)
    values.finish(0)
    values.begin(1)
    tops_max.turn()
    columns(0, tokens, 1024, 1)
    values.relay(1)
    rows_ahead(64)
    tops = tops_max.finish()
    for k in (2, 3):
        size = tops[k - 2 : k - 1, :] / 7.0 + EPS_SCALE
        pair[core, k] = fake_quant(matrix(k), size).astype(jnp.bfloat16)
    spot = pair.at[core, pl.ds(2, 2)]
    swapped = swap(spot, spot, 2)
    values.finish(1)
    values.begin(2, 0)
    swapped.wait()
    combine(2)
    outputs.begin(0)
    rows_ahead(192)
    values.relay(2, 0)
    outputs.finish(0)
    outputs.begin(1)
    values.begin(2, 1)
    rows_ahead(256)
    values.finish(2, 0)
    outputs.relay(1)
    rows_ahead(256)
    values.relay(2, 1)
    outputs.finish(1)
    outputs.begin(2, 0)
    outputs.begin(2, 1)
    values.drain()
    values.drain(0)

    def live_rows(first, count):
        return first + lax.broadcasted_iota(jnp.int32, (count, 1), 0) < own_len

    def mix_block(first, which):
        rows = pl.ds(pl.multiple_of(first, ROW_STEP), ROW_STEP)
        block = lax.dot_general(
            act[rows, :], weights(which), (((1,), (1,)), ((), ())), preferred_element_type=jnp.float32
        )
        mixed[rows, :] = block
        seen = jnp.where(live_rows(first, ROW_STEP), jnp.abs(block), 0.0)
        top[...] = jnp.maximum(top[...], jnp.max(seen.reshape(ROW_STEP // 8, 8, channels), axis=0))

    def set_steps(vrange):
        sizes = CLIP_RATIO * vrange / 7.0 + EPS_SCALE
        step_size[...] = sizes
        gain[...] = 1.0 / sizes

    top[...] = jnp.zeros_like(top)
    loss[...] = square[...] * error[...]
    blocks = tokens // ROW_STEP

    def first(index, carry):
        mix_block(index * ROW_STEP, 0)
        return carry

    lax.fori_loop(0, blocks, first, 0)
    ranges[0].start(jnp.max(top[...], axis=0, keepdims=True))
    values.finish(2, 1)
    outputs.relay(2, 0)
    ranges[0].turn()
    outputs.relay(2, 1)
    outputs.finish(2, 0)
    set_steps(ranges[0].finish())
    values.drain(1)
    outputs.drain()
    outputs.drain(0)
    top[...] = jnp.zeros_like(top)

    def middle(index, carry):
        first = index * ROW_STEP
        rows = pl.ds(pl.multiple_of(first, ROW_STEP), ROW_STEP)
        quantize_mixed(mixed, gain, step_size, mix, error, first, ROW_STEP)
        loss[rows, :] = loss[rows, :] + square[rows, :] * error[rows, :]
        product[rows, :] = product[rows, :] + jnp.dot(mix[rows, :], weights(2), preferred_element_type=jnp.float32)
        quantize_rows(product, act, square, error, first, ROW_STEP)
        loss[rows, :] = loss[rows, :] + square[rows, :] * error[rows, :]
        mix_block(first, 1)
        return carry

    lax.fori_loop(0, 1, middle, 0)
    outputs.finish(2, 1)
    lax.fori_loop(1, blocks, middle, 0)
    ranges[1].start(jnp.max(top[...], axis=0, keepdims=True))
    outputs.drain(1)
    ranges[1].turn()
    set_steps(ranges[1].finish())
    quantize_mixed(mixed, gain, step_size, mix, error, 0, tokens)
    kept = jnp.where(live_rows(0, tokens), loss[...] + square[...] * error[...], 0.0)
    loss_sum.start(jnp.broadcast_to(jnp.sum(kept, axis=0, keepdims=True), sum_ref.shape))

    def store(index):
        rows = pl.ds(pl.multiple_of(index * ROW_STEP, ROW_STEP), ROW_STEP)
        return pltpu.make_async_copy(act.at[rows], out_ref.at[rows], local.at[1 + index])

    def last(index, carry):
        first = index * ROW_STEP
        rows = pl.ds(pl.multiple_of(first, ROW_STEP), ROW_STEP)
        updated = product[rows, :] + jnp.dot(mix[rows, :], weights(3), preferred_element_type=jnp.float32)
        act[rows, :] = jnp.where(live_rows(first, ROW_STEP), updated, 0.0).astype(jnp.bfloat16)
        store(index).start()
        return carry

    lax.fori_loop(0, 1, last, 0)
    loss_sum.turn()
    lax.fori_loop(1, blocks, last, 0)
    count = jnp.sum(all_len_ref[...].astype(jnp.float32), axis=1, keepdims=True)
    sum_ref[...] = loss_sum.finish() / count
    for index in range(blocks):
        store(index).wait()


def per_device(hidden, rotation, norm_gain, value_weight, output_weight, lengths):
    tokens, width = hidden.shape
    layers, part = output_weight.shape[0], output_weight.shape[1]
    channels = part * lax.axis_size(DP)
    shard = rotation.shape[0]
    column = pltpu.VMEM((tokens, 1), jnp.float32)
    cube = (RING, RING, RING)
    dma = pltpu.SemaphoreType.DMA
    scratch = [
        pltpu.VMEM(cube + (2 * shard, width), jnp.bfloat16),
        pltpu.VMEM(cube + (4 * layers * part, width), jnp.bfloat16),
        pltpu.VMEM((tokens + 2 * layers * part, width), jnp.float32),
        pltpu.VMEM((tokens + 2 * layers * part, width), jnp.bfloat16),
        pltpu.VMEM((tokens, channels), jnp.float32),
        pltpu.VMEM((tokens, channels), jnp.bfloat16),
        pltpu.VMEM((2, 2 * layers, part, width), jnp.bfloat16),
        pltpu.VMEM((2, shard, width), jnp.bfloat16),
        column, column, column,
        pltpu.VMEM((8, channels), jnp.float32),
        pltpu.VMEM((1, channels), jnp.float32),
        pltpu.VMEM((1, channels), jnp.float32),
        dma((2, gather_slots(1))), dma((2, gather_slots(1))),
        dma((2, gather_slots(2))), dma((2, gather_slots(2))),
        dma((3,)), dma((3,)), dma((1 + tokens // ROW_STEP,)),
    ]
    for shape in ((layers, width), (1, channels), (1, channels), (1, 128)):
        scratch = scratch + exchange_scratch(shape)
    vmem = pl.BlockSpec(memory_space=pltpu.VMEM)
    out, total = pl.pallas_call(
        window_kernel,
        out_shape=[
            jax.ShapeDtypeStruct((tokens, width), jnp.bfloat16),
            jax.ShapeDtypeStruct((1, 128), jnp.float32),
        ],
        in_specs=[pl.BlockSpec(memory_space=pltpu.SMEM)] + [vmem] * 5 + [pl.BlockSpec(memory_space=pl.ANY)],
        out_specs=[pl.BlockSpec(memory_space=pl.ANY), vmem],
        scratch_shapes=scratch,
        compiler_params=pltpu.CompilerParams(collective_id=4, has_side_effects=True, vmem_limit_bytes=VMEM_LIMIT),
    )(
        lengths, lengths.reshape(1, -1), rotation, jnp.transpose(value_weight, (0, 2, 1)), norm_gain,
        output_weight, hidden,
    )
    return out, total[0, 0]


def solution(mesh):
    finer = Mesh(mesh.devices.reshape(4, 4, 4, 2), DP)
    in_specs = (P(DP, None), P(DP, None), P(), P(None, None, DP), P(None, DP, None), P())
    out_specs = (P(DP, None), P())
    return jax.shard_map(per_device, mesh=finer, in_specs=in_specs, out_specs=out_specs, check_vma=False)
```

time: 192 us -> 160 us (0.83)
  Pallas kernels: 180 us -> 153 us
  other arithmetic: 3.11 us -> 0 us
    pallas_call x2 -> x1, Pallas kernels: 180 us -> 153 us  [per_device(): pl.pallas_call(window_kernel, out_shape=[jax.ShapeDtypeStruct((tokens, wi...]
where the time goes in v4:
time: 160 us; the launch traced here: 159 us
  Pallas kernels  153 us (96%)
  local copies, waits for them, and re-layouts  4.29 us (3%)
  between operations  1.81 us (1%)
    pallas_call x1, Pallas kernels, per_device(): pl.pallas_call(window_kernel, out_shape=[jax.ShapeDtypeStruct((tokens, wi...  153 us
    unnamed x3, local copies, waits for them, and re-layouts  4.29 us

profile of v4, /device:TPU:0, one launch (start us, length us, event | category | flops | bytes accessed | tf_op | source)
XLA Modules:
  0.0 159.4 jit_solution(12054526895330690244)
XLA Ops:
  0.6 153.3 %shard_map.77 = (bf16[768,2560]{1,0:T(8,128)(2,1)}, f32[1,128]{1,0:T(1,128)}) custom-call(s32[128]{0:T(128)} %len_ref.1, s32[1,128]{1,0:T(1,128)} %bitcast.5, bf16[20,2560]{1,0:T(8,128)(2,1)} %rotation_ref.1, bf16[2,8,2560]{2,1,0:T(8,128)(2,1)} %bitcast.4, f32[2,2560]{1,0:T(2,128)} %norm_ref.1, bf16[2,8,2560]{2,1,0:T(8,128)(2,1)} %weight_ref.1, ...), custom_call_target="tpu_custom_call" | custom-call | tf_op jit(solution)/shard_map/pallas_call | solution.py:499
  153.9 0.0 copy-start
  153.9 4.3 %copy.10 = bf16[768,2560]{1,0:T(8,128)(2,1)} copy(bf16[768,2560]{1,0:T(8,128)(2,1)} %get-tuple-element.8) | data formatting | bytes 7864320
  158.2 0.0 copy-done
Async XLA Ops:
  153.9 4.3 %copy-start = (f32[1,128]{1,0:T(1,128)S(1)}, f32[1,128]{1,0:T(1,128)}, u32[]{:S(2)}) copy-start(f32[1,128]{1,0:T(1,128)} %get-tuple-element.5) | copy-start | bytes 1540

commit v5 on v4

--- a/solution.py
+++ b/solution.py
@@ -15,7 +15,7 @@
 SOFT = (6.579714691285096, -12.986868668454669, 12.191614515303863, -6.570949514891455, 1.970640660123473)
 ROW_STEP = 256
 SUB = 64
-VMEM_LIMIT = 63 * 1024 * 1024
+VMEM_LIMIT = 58 * 1024 * 1024
 MESH_ID = pl.DeviceIdType.MESH
 
 
@@ -38,31 +38,30 @@
 
 
 class Gather:
-    def __init__(self, buffer, place, send, recv, first_row, rows, parts, first_column, widths):
+    def __init__(self, buffer, place, send, recv, areas, parts):
         self.buffer, self.place, self.send, self.recv = buffer, place, send, recv
         self.half = buffer.shape[4] // 2
-        self.first_row, self.rows, self.parts = first_row, rows, parts
-        self.first_column, self.widths = first_column, widths
+        self.areas, self.parts = areas, parts
         self.partner = {DP[3]: 1 - place[3]}
         self.pending = {None: []}
         self.state = {}
         self.counter = 0
 
     def view(self, color, position, phase, part, side=None):
-        order = COLORS[color]
+        which, first_row, count, start, width = self.areas[color]
+        order = COLORS[which]
         done = order[:phase]
-        start = self.first_column + sum(self.widths[:color])
-        cols = pl.ds(pl.multiple_of(self.place[3] * self.half + start, 128), self.widths[color])
+        cols = pl.ds(pl.multiple_of(self.place[3] * self.half + start, 128), width)
         index = [self.place[k] for k in range(3)]
         for k in done:
             index[k] = slice(None)
         index[order[phase]] = position
         if side is not None:
             index[done[0]] = pl.ds(2 * side, 2)
-        rows = pl.ds(self.first_row, self.rows)
+        rows = pl.ds(first_row, count)
         if part is not None:
-            count = self.rows // self.parts
-            rows = pl.ds(self.first_row + part * count, count)
+            count = count // self.parts
+            rows = pl.ds(first_row + part * count, count)
         return self.buffer.at[index[0], index[1], index[2], rows, cols]
 
     def copy(self, view, peer, part):
@@ -77,12 +76,12 @@
         return copy
 
     def ring(self, color, phase):
-        axis = COLORS[color][phase]
+        axis = COLORS[self.areas[color][0]][phase]
         own = self.place[axis]
         return axis, own, lax.rem(own + 1, RING), lax.rem(own + 2, RING), lax.rem(own + RING - 1, RING)
 
     def begin(self, phase, part=None):
-        for color in range(3):
+        for color in range(len(self.areas)):
             axis, own, above, across, below = self.ring(color, phase)
             block = self.view(color, own, phase, part)
             copies = [self.copy(block, {DP[axis]: above}, part), self.copy(block, {DP[axis]: below}, part)]
@@ -91,7 +90,7 @@
             self.state[phase, color, part] = copies
 
     def relay(self, phase, part=None):
-        for color in range(3):
+        for color in range(len(self.areas)):
             axis, own, above, across, below = self.ring(color, phase)
             from_below, from_above = self.state[phase, color, part]
             from_below.wait_recv()
@@ -103,7 +102,7 @@
             self.state[phase, color, part] = [first, second]
 
     def finish(self, phase, part=None):
-        for color in range(3):
+        for color in range(len(self.areas)):
             axis, own, above, across, below = self.ring(color, phase)
             for copy in self.state[phase, color, part]:
                 copy.wait_recv()
@@ -119,8 +118,14 @@
                 copy.wait_recv()
 
 
-def gather_slots(parts):
-    return 3 * (6 + 7 + 7 * parts)
+def bands(first_row, rows, first_column, widths):
+    return [
+        (k, first_row, rows, first_column + sum(widths[:k]), width) for k, width in enumerate(widths)
+    ]
+
+
+def gather_slots(areas, parts):
+    return areas * (6 + 7 + 7 * parts)
 
 
 NEAR = [(dy, dc) for dy in range(4) for dc in range(2) if (dy, dc) != (0, 0)]
@@ -189,13 +194,13 @@
     ]
 
 
-def quantize_rows(resid, act, square, error, first, count):
+def quantize_rows(resid, act, square, error, first, count, sub=SUB):
     width = resid.shape[1]
 
     def step(index, carry):
-        rows = pl.ds(pl.multiple_of(first + index * SUB, SUB), SUB)
-        squares = jnp.zeros((SUB, 128), jnp.float32)
-        tops = jnp.zeros((SUB, 128), jnp.float32)
+        rows = pl.ds(pl.multiple_of(first + index * sub, sub), sub)
+        squares = jnp.zeros((sub, 128), jnp.float32)
+        tops = jnp.zeros((sub, 128), jnp.float32)
         for start in range(0, width, 128):
             part = resid[rows, start : start + 128]
             squares = squares + part * part
@@ -203,9 +208,9 @@
         mean_sq = jnp.sum(squares, axis=1, keepdims=True) / width
         scale = lax.rsqrt(mean_sq + EPS_NORM)
         step_size = CLIP_RATIO * (jnp.max(tops, axis=1, keepdims=True) * scale) / 7.0 + EPS_SCALE
-        gain = jnp.broadcast_to(scale / step_size, (SUB, 128))
-        wide_step = jnp.broadcast_to(step_size, (SUB, 128))
-        errors = jnp.zeros((SUB, 128), jnp.float32)
+        gain = jnp.broadcast_to(scale / step_size, (sub, 128))
+        wide_step = jnp.broadcast_to(step_size, (sub, 128))
+        errors = jnp.zeros((sub, 128), jnp.float32)
         for start in range(0, width, 128):
             units = resid[rows, start : start + 128] * gain
             rounded = soft_round(jnp.minimum(jnp.maximum(units, -8.0), 7.0))
@@ -216,15 +221,15 @@
         error[rows, :] = jnp.sum(errors, axis=1, keepdims=True) * (step_size * step_size)
         return carry
 
-    lax.fori_loop(0, count // SUB, step, 0)
-
-
-def quantize_mixed(mixed, gain, step_size, mix, error, first, count):
+    lax.fori_loop(0, count // sub, step, 0)
+
+
+def quantize_mixed(mixed, gain, step_size, mix, error, first, count, sub=SUB):
     channels = mixed.shape[1]
 
     def step(index, carry):
-        rows = pl.ds(pl.multiple_of(first + index * SUB, SUB), SUB)
-        errors = jnp.zeros((SUB, 128), jnp.float32)
+        rows = pl.ds(pl.multiple_of(first + index * sub, sub), sub)
+        errors = jnp.zeros((sub, 128), jnp.float32)
         for start in range(0, channels, 128):
             cols = slice(start, start + 128)
             units = mixed[rows, cols] * gain[:, cols]
@@ -235,7 +240,7 @@
         error[rows, :] = jnp.sum(errors, axis=1, keepdims=True)
         return carry
 
-    lax.fori_loop(0, count // SUB, step, 0)
+    lax.fori_loop(0, count // sub, step, 0)
 
 
 def window_kernel(
@@ -282,8 +287,13 @@
     turn[place[0], place[1], place[2]] = jnp.concatenate(
         [both_shards[0].astype(jnp.float32), both_shards[1].astype(jnp.float32)], axis=0
     ).astype(jnp.bfloat16)
-    early = Gather(turn, place, turn_send.at[0], turn_recv.at[0], 0, 2 * shard, 1, 0, (256, 256, 256))
-    late = Gather(turn, place, turn_send.at[1], turn_recv.at[1], 0, 2 * shard, 1, 768, (256, 128, 128))
+    early = Gather(turn, place, turn_send.at[0], turn_recv.at[0], bands(0, 2 * shard, 0, (256, 256, 256)), 1)
+    third = (2 * shard // 3 + 7) // 8 * 8
+    slices = [(0, 0, third), (1, third, third), (2, 2 * third, 2 * shard - 2 * third)]
+    shared = [(which, row, rows, 1152, 128) for which, row, rows in slices]
+    late = Gather(
+        turn, place, turn_send.at[1], turn_recv.at[1], bands(0, 2 * shard, 768, (128, 128, 128)) + shared, 1
+    )
     chunk = 256
 
     def columns(first_row, rows, first, count):
@@ -315,8 +325,9 @@
     early.finish(2)
     early.drain()
     late.relay(2)
-    columns(0, tokens + 4 * part, 0, 3)
+    columns(0, tokens + 4 * part, 0, 2)
     late.finish(2)
+    columns(0, tokens + 4 * part, 512, 1)
     late.drain()
     columns(tokens, 4 * part, 768, 2)
 
@@ -348,8 +359,9 @@
     spot = pair.at[core, pl.ds(0, 2)]
     swapped = swap(spot, spot, 1)
     tops_max.start(output_tops)
-    values = Gather(full, place, ring_send.at[0], ring_recv.at[0], 0, 4 * part, 2, 0, (512, 384, 384))
-    outputs = Gather(full, place, ring_send.at[1], ring_recv.at[1], 4 * part, 4 * part, 2, 0, (384, 512, 384))
+    wide_first, wide_second = (512, 384, 384), (384, 512, 384)
+    values = Gather(full, place, ring_send.at[0], ring_recv.at[0], bands(0, 4 * part, 0, wide_first), 2)
+    outputs = Gather(full, place, ring_send.at[1], ring_recv.at[1], bands(4 * part, 4 * part, 0, wide_second), 2)
     swapped.wait()
     combine(0)
     values.begin(0)
@@ -367,23 +379,22 @@
     spot = pair.at[core, pl.ds(2, 2)]
     swapped = swap(spot, spot, 2)
     values.finish(1)
-    values.begin(2, 0)
     swapped.wait()
     combine(2)
     outputs.begin(0)
+    values.begin(2, 0)
+    rows_ahead(192)
+    outputs.finish(0)
+    outputs.begin(1)
     rows_ahead(192)
     values.relay(2, 0)
-    outputs.finish(0)
-    outputs.begin(1)
+    rows_ahead(64)
+    outputs.relay(1)
     values.begin(2, 1)
     rows_ahead(256)
     values.finish(2, 0)
-    outputs.relay(1)
-    rows_ahead(256)
-    values.relay(2, 1)
     outputs.finish(1)
     outputs.begin(2, 0)
-    outputs.begin(2, 1)
     values.drain()
     values.drain(0)
 
@@ -412,12 +423,14 @@
         mix_block(index * ROW_STEP, 0)
         return carry
 
-    lax.fori_loop(0, blocks, first, 0)
+    lax.fori_loop(0, blocks - 1, first, 0)
+    values.relay(2, 1)
+    lax.fori_loop(blocks - 1, blocks, first, 0)
     ranges[0].start(jnp.max(top[...], axis=0, keepdims=True))
+    ranges[0].turn()
+    outputs.relay(2, 0)
     values.finish(2, 1)
-    outputs.relay(2, 0)
-    ranges[0].turn()
-    outputs.relay(2, 1)
+    outputs.begin(2, 1)
     outputs.finish(2, 0)
     set_steps(ranges[0].finish())
     values.drain(1)
@@ -428,35 +441,31 @@
     def middle(index, carry):
         first = index * ROW_STEP
         rows = pl.ds(pl.multiple_of(first, ROW_STEP), ROW_STEP)
-        quantize_mixed(mixed, gain, step_size, mix, error, first, ROW_STEP)
+        quantize_mixed(mixed, gain, step_size, mix, error, first, ROW_STEP, 128)
         loss[rows, :] = loss[rows, :] + square[rows, :] * error[rows, :]
         product[rows, :] = product[rows, :] + jnp.dot(mix[rows, :], weights(2), preferred_element_type=jnp.float32)
-        quantize_rows(product, act, square, error, first, ROW_STEP)
+        quantize_rows(product, act, square, error, first, ROW_STEP, 128)
         loss[rows, :] = loss[rows, :] + square[rows, :] * error[rows, :]
         mix_block(first, 1)
         return carry
 
     lax.fori_loop(0, 1, middle, 0)
+    outputs.relay(2, 1)
+    lax.fori_loop(1, blocks, middle, 0)
     outputs.finish(2, 1)
-    lax.fori_loop(1, blocks, middle, 0)
     ranges[1].start(jnp.max(top[...], axis=0, keepdims=True))
     outputs.drain(1)
     ranges[1].turn()
     set_steps(ranges[1].finish())
-    quantize_mixed(mixed, gain, step_size, mix, error, 0, tokens)
+    quantize_mixed(mixed, gain, step_size, mix, error, 0, tokens, 128)
     kept = jnp.where(live_rows(0, tokens), loss[...] + square[...] * error[...], 0.0)
     loss_sum.start(jnp.broadcast_to(jnp.sum(kept, axis=0, keepdims=True), sum_ref.shape))
-
-    def store(index):
-        rows = pl.ds(pl.multiple_of(index * ROW_STEP, ROW_STEP), ROW_STEP)
-        return pltpu.make_async_copy(act.at[rows], out_ref.at[rows], local.at[1 + index])
 
     def last(index, carry):
         first = index * ROW_STEP
         rows = pl.ds(pl.multiple_of(first, ROW_STEP), ROW_STEP)
         updated = product[rows, :] + jnp.dot(mix[rows, :], weights(3), preferred_element_type=jnp.float32)
-        act[rows, :] = jnp.where(live_rows(first, ROW_STEP), updated, 0.0).astype(jnp.bfloat16)
-        store(index).start()
+        out_ref[rows, :] = jnp.where(live_rows(first, ROW_STEP), updated, 0.0).astype(jnp.bfloat16)
         return carry
 
     lax.fori_loop(0, 1, last, 0)
@@ -464,8 +473,6 @@
     lax.fori_loop(1, blocks, last, 0)
     count = jnp.sum(all_len_ref[...].astype(jnp.float32), axis=1, keepdims=True)
     sum_ref[...] = loss_sum.finish() / count
-    for index in range(blocks):
-        store(index).wait()
 
 
 def per_device(hidden, rotation, norm_gain, value_weight, output_weight, lengths):
@@ -489,9 +496,9 @@
         pltpu.VMEM((8, channels), jnp.float32),
         pltpu.VMEM((1, channels), jnp.float32),
         pltpu.VMEM((1, channels), jnp.float32),
-        dma((2, gather_slots(1))), dma((2, gather_slots(1))),
-        dma((2, gather_slots(2))), dma((2, gather_slots(2))),
-        dma((3,)), dma((3,)), dma((1 + tokens // ROW_STEP,)),
+        dma((2, gather_slots(6, 1))), dma((2, gather_slots(6, 1))),
+        dma((2, gather_slots(3, 2))), dma((2, gather_slots(3, 2))),
+        dma((3,)), dma((3,)), dma((1,)),
     ]
     for shape in ((layers, width), (1, channels), (1, channels), (1, 128)):
         scratch = scratch + exchange_scratch(shape)
@@ -499,11 +506,11 @@
     out, total = pl.pallas_call(
         window_kernel,
         out_shape=[
-            jax.ShapeDtypeStruct((tokens, width), jnp.bfloat16),
-            jax.ShapeDtypeStruct((1, 128), jnp.float32),
+            pltpu.VMEM((tokens, width), jnp.bfloat16),
+            pltpu.VMEM((1, 128), jnp.float32),
         ],
         in_specs=[pl.BlockSpec(memory_space=pltpu.SMEM)] + [vmem] * 5 + [pl.BlockSpec(memory_space=pl.ANY)],
-        out_specs=[pl.BlockSpec(memory_space=pl.ANY), vmem],
+        out_specs=[vmem, vmem],
         scratch_shapes=scratch,
         compiler_params=pltpu.CompilerParams(collective_id=4, has_side_effects=True, vmem_limit_bytes=VMEM_LIMIT),
     )(

time: 160 us -> 152 us (0.950)
  Pallas kernels: 153 us -> 148 us
  local copies, waits for them, and re-layouts: 4.29 us -> 1.93 us
    pallas_call x1, Pallas kernels: 153 us -> 148 us  [per_device(): pl.pallas_call(window_kernel, out_shape=[pltpu.VMEM((tokens, width), jnp....]
    unnamed x3 -> x1, local copies, waits for them, and re-layouts: 4.29 us -> 1.93 us
where the time goes in v5:
time: 152 us
  Pallas kernels  148 us (97%)
  local copies, waits for them, and re-layouts  1.93 us (1%)
  between operations  1.81 us (1%)
    pallas_call x1, Pallas kernels, per_device(): pl.pallas_call(window_kernel, out_shape=[pltpu.VMEM((tokens, width), jnp....  148 us

profile of v5, /device:TPU:0, one launch (start us, length us, event | category | flops | bytes accessed | tf_op | source)
XLA Modules:
  0.0 151.8 jit_solution(7968761957014532174)
XLA Ops:
  0.6 148.1 %shard_map.77 = (bf16[768,2560]{1,0:T(8,128)(2,1)S(1)}, f32[1,128]{1,0:T(1,128)S(1)}) custom-call(s32[128]{0:T(128)} %len_ref.1, s32[1,128]{1,0:T(1,128)} %bitcast.6, bf16[20,2560]{1,0:T(8,128)(2,1)} %rotation_ref.1, bf16[2,8,2560]{2,1,0:T(8,128)(2,1)} %bitcast.5, f32[2,2560]{1,0:T(2,128)} %norm_ref.1, bf16[2,8,2560]{2,1,0:T(8,128)(2,1)} %weight_ref.1, ...), custom_call_target="tpu_custom_call" | custom-call | tf_op jit(solution)/shard_map/pallas_call | solution.py:506
  148.7 1.9 %copy.10 = bf16[768,2560]{1,0:T(8,128)(2,1)} copy(bf16[768,2560]{1,0:T(8,128)(2,1)S(1)} %get-tuple-element.6) | data formatting | bytes 7864320

commit v6 on v5

--- a/solution.py
+++ b/solution.py
@@ -423,14 +423,13 @@
         mix_block(index * ROW_STEP, 0)
         return carry
 
-    lax.fori_loop(0, blocks - 1, first, 0)
+    lax.fori_loop(0, blocks, first, 0)
+    ranges[0].start(jnp.max(top[...], axis=0, keepdims=True))
     values.relay(2, 1)
-    lax.fori_loop(blocks - 1, blocks, first, 0)
-    ranges[0].start(jnp.max(top[...], axis=0, keepdims=True))
     ranges[0].turn()
     outputs.relay(2, 0)
+    outputs.begin(2, 1)
     values.finish(2, 1)
-    outputs.begin(2, 1)
     outputs.finish(2, 0)
     set_steps(ranges[0].finish())
     values.drain(1)

time: 152 us -> 150 us (0.987)
  Pallas kernels: 148 us -> 146 us
    pallas_call x1, Pallas kernels: 148 us -> 146 us  [per_device(): pl.pallas_call(window_kernel, out_shape=[pltpu.VMEM((tokens, width), jnp....]
where the time goes in v6:
time: 150 us
  Pallas kernels  146 us (97%)
  local copies, waits for them, and re-layouts  1.93 us (1%)
  between operations  1.81 us (1%)
    pallas_call x1, Pallas kernels, per_device(): pl.pallas_call(window_kernel, out_shape=[pltpu.VMEM((tokens, width), jnp....  146 us

profile of v6, /device:TPU:0, one launch (start us, length us, event | category | flops | bytes accessed | tf_op | source)
XLA Modules:
  0.0 150.2 jit_solution(606948084494310951)
XLA Ops:
  0.6 146.4 %shard_map.77 = (bf16[768,2560]{1,0:T(8,128)(2,1)S(1)}, f32[1,128]{1,0:T(1,128)S(1)}) custom-call(s32[128]{0:T(128)} %len_ref.1, s32[1,128]{1,0:T(1,128)} %bitcast.6, bf16[20,2560]{1,0:T(8,128)(2,1)} %rotation_ref.1, bf16[2,8,2560]{2,1,0:T(8,128)(2,1)} %bitcast.5, f32[2,2560]{1,0:T(2,128)} %norm_ref.1, bf16[2,8,2560]{2,1,0:T(8,128)(2,1)} %weight_ref.1, ...), custom_call_target="tpu_custom_call" | custom-call | tf_op jit(solution)/shard_map/pallas_call | solution.py:505
  147.1 1.9 %copy.10 = bf16[768,2560]{1,0:T(8,128)(2,1)} copy(bf16[768,2560]{1,0:T(8,128)(2,1)S(1)} %get-tuple-element.6) | data formatting | bytes 7864320
